TPU v7x, 32 devices: a whole 2x2x4 slice. The times are simulated.
32 devices in a mesh: rel: 4 (over z), node: 2 (over x), head: 4 (over y, core).
Axes of the slice: x: 2, y: 2, z: 4, core: 2. Of those that a mesh axis runs over, the one named last changes fastest.
Arguments:
- features: bfloat16 [4096, 512], P('node'), may hold values from -26 to 26
- node_type: int32 [4096], P('node'), may hold values from 0 to 3
- w_query: bfloat16 [4, 512, 512], P(None, None, 'head'), may hold values from -0.25 to 0.25
- w_key: bfloat16 [4, 512, 512], P(None, None, 'head'), may hold values from -0.25 to 0.25
- w_value: bfloat16 [4, 512, 512], P(None, None, 'head'), may hold values from -0.25 to 0.25
- rel_att: bfloat16 [64, 8, 64, 64], P(None, 'head'), may hold values from -0.75 to 0.75
- rel_msg: bfloat16 [64, 8, 64, 64], P(None, 'head'), may hold values from -0.75 to 0.75
- rel_prior: float32 [64, 8], P(None, 'head'), may hold values from 0.5 to 3
- w_out: bfloat16 [4, 512, 512], P(None, 'head'), may hold values from -0.25 to 0.25
- skip: float32 [4], replicated, may hold values from -1.5 to 1.5
- rel_perm: int32 [64], P('rel'), may hold values from 0 to 63, each once
- tile_src: int32 [64, 32], P('rel', 'node'), may hold values from 0 to 31
- tile_dst: int32 [64, 32], P('rel', 'node'), may hold values from 0 to 15
- tile_bits: int32 [64, 32, 128, 4], P('rel', 'node'), may hold values from -2147483648 to 2147483646
- tile_count: int32 [64, 2], P('rel', 'node'), may hold values from 1 to 16, as said below
Outputs:
- updated: bfloat16 [4096, 512], P(('node', 'head'))
Inputs may be any that keep to these rules, and one draw needn't show every extreme that they name: The first tile_count[p, g] slots of group g of position p are live; the words of the other slots may have bits set, but those bits give no edges and must be ignored. Some position has all 16 slots live in every group.
All inputs are finite; a program needn't handle non-finite values.
Results may differ from a plain program's by a relative error of at most 0.008.
The roundings to bfloat16 on the way count: a program that leaves them out, or rounds other values in their place, can miss the bound.
Values may be sent and summed in bfloat16 or wider, within the bound.
No kernel may reach another device: no remote copies, remote signals or barrier semaphores. Data moves between devices by JAX's collectives and lax.ppermute only.
A program may use at most 128 MiB of HBM per device.

v0:
```python
import math

import jax
import jax.numpy as jnp
from jax import lax
from jax.sharding import PartitionSpec as P

NEG = -1e30


def project(rows, types, weights):
    total = jnp.zeros((rows.shape[0], weights.shape[2]), jnp.float32)
    for kind in range(weights.shape[0]):
        partial_out = jnp.dot(rows, weights[kind], preferred_element_type=jnp.float32)
        total = jnp.where((types == kind)[:, None], partial_out, total)
    return total


def unpack(words):
    shifts = jnp.arange(32, dtype=jnp.int32)
    bits = words[..., None] >> shifts & 1
    return bits.reshape(words.shape[:-1] + (words.shape[-1] * 32,)) > 0


def gate_of(kinds, skip):
    table = jax.nn.sigmoid(skip)
    hits = kinds[:, None] == jnp.arange(skip.shape[0], dtype=jnp.int32)[None, :]
    return jnp.sum(jnp.where(hits, table[None, :], 0.0), axis=1)[:, None]


def per_device(
    features,
    node_type,
    w_query,
    w_key,
    w_value,
    rel_att,
    rel_msg,
    rel_prior,
    w_out,
    skip,
    rel_perm,
    tile_src,
    tile_dst,
    tile_bits,
    tile_count,
):
    node_rows = features.shape[0]
    n_rel = lax.axis_size("rel")
    n_node = lax.axis_size("node")
    n_head = lax.axis_size("head")
    heads = rel_prior.shape[1]
    cols = w_query.shape[2]
    head_size = cols // heads
    block = tile_bits.shape[2]
    words = tile_bits.shape[3]
    blocks = node_rows // block
    query = project(features, node_type, w_query).astype(jnp.bfloat16)
    quarter = node_rows // n_rel
    per_quarter = quarter // block
    first_row = lax.axis_index("rel") * quarter
    own_rows = lax.dynamic_slice_in_dim(features, first_row, quarter, 0)
    own_kinds = lax.dynamic_slice_in_dim(node_type, first_row, quarter, 0)
    keys_own = project(own_rows, own_kinds, w_key).astype(jnp.bfloat16)
    values_own = project(own_rows, own_kinds, w_value).astype(jnp.bfloat16)
    keys_all, values_all = (
        lax.all_gather(keys_own, ("rel", "node"), axis=0, tiled=True),
        lax.all_gather(values_own, ("rel", "node"), axis=0, tiled=True),
    )

    def locate(src):
        local_block = src % blocks
        return (
            local_block // per_quarter * (n_node * per_quarter)
            + src // blocks * per_quarter
            + local_block % per_quarter
        )

    key_blocks = keys_all.reshape(-1, block, cols)
    value_blocks = values_all.reshape(-1, block, cols)
    query_blocks = query.reshape(blocks, block, cols)
    factor = 1.0 / math.sqrt(head_size)
    att = rel_att[rel_perm]
    msg_w = rel_msg[rel_perm]
    prior = rel_prior[rel_perm] * factor
    tcap = tile_src.shape[1]
    slots = tile_src.shape[0] * tcap
    flat_src = tile_src.reshape(slots)
    flat_dst = tile_dst.reshape(slots)
    flat_bits = tile_bits.reshape(slots, block, words)
    slot_ids = jnp.arange(slots, dtype=jnp.int32)
    live = slot_ids % tcap < tile_count[slot_ids // tcap, 0]
    order = jnp.argsort(jnp.where(live, 0, 1).astype(jnp.int32), stable=True)
    live_count = jnp.sum(live.astype(jnp.int32))
    group = math.gcd(32, slots)
    turns = (live_count + group - 1) // group

    def visit(turn, carry):
        m_run, l_run, acc = carry
        picks = lax.dynamic_slice_in_dim(order, turn * group, group, 0)
        valid = turn * group + jnp.arange(group, dtype=jnp.int32) < live_count
        position = picks // tcap
        src = locate(flat_src[picks])
        dst = flat_dst[picks]
        q_rows = query_blocks[dst].reshape(group, block, heads, head_size)
        k_tiles = key_blocks[src].reshape(group, block, heads, head_size)
        v_tiles = value_blocks[src].reshape(group, block, heads, head_size)
        q_tiles = (
            jnp.einsum("gihe,ghde->gihd", q_rows, att[position], preferred_element_type=jnp.float32)
            * prior[position][:, None, :, None]
        ).astype(jnp.bfloat16)
        message = jnp.einsum(
            "gjhd,ghde->gjhe", v_tiles, msg_w[position], preferred_element_type=jnp.float32
        ).astype(jnp.bfloat16)
        scores = jnp.einsum("gihd,gjhd->ghij", q_tiles, k_tiles, preferred_element_type=jnp.float32)
        edges = unpack(flat_bits[picks]) & valid[:, None, None]
        masked = jnp.where(edges[:, None], scores, NEG)
        tile_top = masked.max(-1)
        m_new = m_run.at[dst].max(tile_top)
        weights = jnp.where(edges[:, None], jnp.exp(masked - m_new[dst][..., None]), 0.0)
        rescale = jnp.exp(m_run - m_new)
        l_new = (l_run * rescale).at[dst].add(weights.sum(-1))
        weighted = jnp.einsum(
            "ghij,gjhe->gihe",
            weights.astype(jnp.bfloat16),
            message,
            preferred_element_type=jnp.float32,
        )
        weighted = weighted.reshape(group, block, cols)
        spread = jnp.repeat(rescale.transpose(0, 2, 1), head_size, axis=2)
        acc_new = (acc * spread).at[dst].add(weighted)
        return (m_new, l_new, acc_new)

    init = (
        jnp.full((blocks, heads, block), NEG, jnp.float32),
        jnp.zeros((blocks, heads, block), jnp.float32),
        jnp.zeros((blocks, block, cols), jnp.float32),
    )
    m_run, l_run, acc = lax.fori_loop(0, turns, visit, init)
    m_rows = m_run.transpose(0, 2, 1).reshape(node_rows, heads)
    l_rows = l_run.transpose(0, 2, 1).reshape(node_rows, heads)
    acc_rows = acc.reshape(node_rows, cols)
    top = lax.pmax(m_rows, "rel")
    scaling = jnp.exp(m_rows - top)
    l_scaled = l_rows * scaling
    a_scaled = acc_rows * jnp.repeat(scaling, head_size, axis=1)
    piece = node_rows // (n_rel * n_head)

    def regroup(arr):
        return (
            arr.reshape(n_head, n_rel, piece, arr.shape[1])
            .transpose(1, 0, 2, 3)
            .reshape(node_rows, arr.shape[1])
        )

    a_sum, l_sum = (
        lax.psum_scatter(
            regroup(a_scaled).astype(jnp.bfloat16), "rel", scatter_dimension=0, tiled=True
        ).astype(jnp.float32),
        lax.psum_scatter(
            regroup(l_scaled).astype(jnp.bfloat16), "rel", scatter_dimension=0, tiled=True
        ).astype(jnp.float32),
    )
    kinds_grouped = node_type.reshape(n_head, n_rel, piece).transpose(1, 0, 2).reshape(node_rows)
    kinds_mine = lax.dynamic_slice_in_dim(
        kinds_grouped, lax.axis_index("rel") * n_head * piece, n_head * piece, 0
    )
    hidden = jax.nn.gelu(a_sum / jnp.repeat(jnp.maximum(l_sum, 1.0), head_size, axis=1)).astype(
        jnp.bfloat16
    )
    mixed = lax.psum_scatter(
        project(hidden, kinds_mine, w_out).astype(jnp.bfloat16),
        "head",
        scatter_dimension=0,
        tiled=True,
    ).astype(jnp.float32)
    first_row = (lax.axis_index("head") * n_rel + lax.axis_index("rel")) * piece
    resid = lax.dynamic_slice_in_dim(features, first_row, piece, 0).astype(jnp.float32)
    kinds = lax.dynamic_slice_in_dim(node_type, first_row, piece, 0)
    gate = gate_of(kinds, skip)
    finished = (gate * mixed + (1.0 - gate) * resid).astype(jnp.bfloat16)
    return lax.all_gather(finished, "rel", axis=0, tiled=True)


def solution(mesh):
    in_specs = (
        P("node", None),
        P("node"),
        P(None, None, "head"),
        P(None, None, "head"),
        P(None, None, "head"),
        P(None, "head", None, None),
        P(None, "head", None, None),
        P(None, "head"),
        P(None, "head", None),
        P(),
        P("rel"),
        P("rel", "node"),
        P("rel", "node"),
        P("rel", "node", None, None),
        P("rel", "node"),
    )
    out_specs = P(("node", "head"), None)
    return jax.shard_map(
        per_device, mesh=mesh, in_specs=in_specs, out_specs=out_specs, check_vma=False
    )
```

profile of v0, /device:TPU:0, one launch (start us, length us, event | category | flops | bytes accessed | tf_op | source)
XLA Modules:
  0.0 494.9 jit_solution(10378340879098127760)
XLA Ops:
  25.5 3.0 gather_fusion.13
  28.5 3.1 sort.17
  38.1 19.3 %all-gather.3.cloned.1.call-done = bf16[4096,128]{1,0:T(8,128)(2,1)} async-done(((bf16[512,128]{1,0:T(8,128)(2,1)}), bf16[4096,128]{1,0:T(8,128)(2,1)}) %all-gather.3.cloned.1.call-update) | async-done | bytes 1048592 | tf_op jit(solution)/shard_map/all_gather | solution.py:67
  57.4 41.1 %all-gather.5.cloned.1.call-done = bf16[4096,128]{1,0:T(8,128)(2,1)} async-done(((bf16[512,128]{1,0:T(8,128)(2,1)}), bf16[4096,128]{1,0:T(8,128)(2,1)}) %all-gather.5.cloned.1.call-update) | async-done | bytes 1048592 | tf_op jit(solution)/shard_map/all_gather | solution.py:68
  98.7 232.6 %while.17 = (s32[]{:T(128)}, f32[16,2,128]{2,1,0:T(2,128)S(1)}, f32[16,2,128]{2,1,0:T(2,128)S(1)}, f32[16,128,128]{2,1,0:T(8,128)S(1)}, s32[]{:T(128)}, /*index=...) while((s32[]{:T(128)}, f32[16,2,128]{2,1,0:T(2,128)S(1)}, ...), condition=%wide.region_9.10_spmd, body=%wide.region_3.9_spmd.sunk | while | flops 417609920 | bytes 53205560 | solution.py:139
  104.2 2.9 gather_fusion.3
  117.8 5.1 %select_reduce_fusion.3 = (f32[32,2,128]{2,1,0:T(2,128)S(1)}, f32[32,2,128,128]{2,3,1,0:T(8,128)}) fusion(pred[32,128,128]{1,2,0:T(8,128)(4,1)} %fusion.126, bf16[32,128,2,64]{1,3,2,0:T(8,128)(2,1)} %bitcast.179, bf16[32,2,64,64]{3,2,1,0:T(8,128)(2,1)} %gather_fusion.4, bf16[32,128,2,64]{1,3,2,0:T(8,128)(2,1)} %bitcast.180, ...), kind=kOutput, calls=%fused_computation.18.clone.1 | convolution fusion | flops 204464128 | bytes 7373056 | tf_op jit(solution)/shard_map/while/body/gihd,gjhd->ghij/dot_general | solution.py:115
  125.2 3.7 fusion.129
  143.6 5.7 %fusion.130 = f32[32,2,64,128]{3,2,1,0:T(8,128)} fusion(f32[32,2,128,128]{2,3,1,0:T(8,128)} %get-tuple-element.438, f32[32,2,128]{2,1,0:T(2,128)S(1)} %gather_fusion.7, pred[32,128,128]{1,2,0:T(8,128)(4,1)} %fusion.126, bf16[32,2,64,64]{3,2,1,0:T(8,128)(2,1)} %gather_fusion.8, bf16[32,128,2,64]{1,3,2,0:T(8,128)(2,1)} %bitcast.186), kind=kOutput, calls=%fused_computation.21.clone.1 | convolution fusion | flops 206045184 | bytes 8421376 | tf_op jit(solution)/shard_map/while/body/ghij,gjhe->gihe/dot_general | solution.py:123
  149.3 2.9 copy.83
  152.3 4.7 scatter_fusion.2
  175.9 5.1 %select_reduce_fusion.3 = (f32[32,2,128]{2,1,0:T(2,128)S(1)}, f32[32,2,128,128]{2,3,1,0:T(8,128)}) fusion(pred[32,128,128]{1,2,0:T(8,128)(4,1)} %fusion.126, bf16[32,128,2,64]{1,3,2,0:T(8,128)(2,1)} %bitcast.179, bf16[32,2,64,64]{3,2,1,0:T(8,128)(2,1)} %gather_fusion.4, bf16[32,128,2,64]{1,3,2,0:T(8,128)(2,1)} %bitcast.180, ...), kind=kOutput, calls=%fused_computation.18.clone.1 | convolution fusion | flops 204464128 | bytes 7373056 | tf_op jit(solution)/shard_map/while/body/gihd,gjhd->ghij/dot_general | solution.py:115
  183.3 3.7 fusion.129
  201.7 5.7 %fusion.130 = f32[32,2,64,128]{3,2,1,0:T(8,128)} fusion(f32[32,2,128,128]{2,3,1,0:T(8,128)} %get-tuple-element.438, f32[32,2,128]{2,1,0:T(2,128)S(1)} %gather_fusion.7, pred[32,128,128]{1,2,0:T(8,128)(4,1)} %fusion.126, bf16[32,2,64,64]{3,2,1,0:T(8,128)(2,1)} %gather_fusion.8, bf16[32,128,2,64]{1,3,2,0:T(8,128)(2,1)} %bitcast.186), kind=kOutput, calls=%fused_computation.21.clone.1 | convolution fusion | flops 206045184 | bytes 8421376 | tf_op jit(solution)/shard_map/while/body/ghij,gjhe->gihe/dot_general | solution.py:123
  207.4 2.9 copy.83
  210.4 4.7 scatter_fusion.2
  234.0 5.1 %select_reduce_fusion.3 = (f32[32,2,128]{2,1,0:T(2,128)S(1)}, f32[32,2,128,128]{2,3,1,0:T(8,128)}) fusion(pred[32,128,128]{1,2,0:T(8,128)(4,1)} %fusion.126, bf16[32,128,2,64]{1,3,2,0:T(8,128)(2,1)} %bitcast.179, bf16[32,2,64,64]{3,2,1,0:T(8,128)(2,1)} %gather_fusion.4, bf16[32,128,2,64]{1,3,2,0:T(8,128)(2,1)} %bitcast.180, ...), kind=kOutput, calls=%fused_computation.18.clone.1 | convolution fusion | flops 204464128 | bytes 7373056 | tf_op jit(solution)/shard_map/while/body/gihd,gjhd->ghij/dot_general | solution.py:115
  241.4 3.7 fusion.129
  259.8 5.7 %fusion.130 = f32[32,2,64,128]{3,2,1,0:T(8,128)} fusion(f32[32,2,128,128]{2,3,1,0:T(8,128)} %get-tuple-element.438, f32[32,2,128]{2,1,0:T(2,128)S(1)} %gather_fusion.7, pred[32,128,128]{1,2,0:T(8,128)(4,1)} %fusion.126, bf16[32,2,64,64]{3,2,1,0:T(8,128)(2,1)} %gather_fusion.8, bf16[32,128,2,64]{1,3,2,0:T(8,128)(2,1)} %bitcast.186), kind=kOutput, calls=%fused_computation.21.clone.1 | convolution fusion | flops 206045184 | bytes 8421376 | tf_op jit(solution)/shard_map/while/body/ghij,gjhe->gihe/dot_general | solution.py:123
  265.5 2.9 copy.83
  268.5 4.7 scatter_fusion.2
  292.1 5.1 %select_reduce_fusion.3 = (f32[32,2,128]{2,1,0:T(2,128)S(1)}, f32[32,2,128,128]{2,3,1,0:T(8,128)}) fusion(pred[32,128,128]{1,2,0:T(8,128)(4,1)} %fusion.126, bf16[32,128,2,64]{1,3,2,0:T(8,128)(2,1)} %bitcast.179, bf16[32,2,64,64]{3,2,1,0:T(8,128)(2,1)} %gather_fusion.4, bf16[32,128,2,64]{1,3,2,0:T(8,128)(2,1)} %bitcast.180, ...), kind=kOutput, calls=%fused_computation.18.clone.1 | convolution fusion | flops 204464128 | bytes 7373056 | tf_op jit(solution)/shard_map/while/body/gihd,gjhd->ghij/dot_general | solution.py:115
  299.5 3.7 fusion.129
  317.9 5.7 %fusion.130 = f32[32,2,64,128]{3,2,1,0:T(8,128)} fusion(f32[32,2,128,128]{2,3,1,0:T(8,128)} %get-tuple-element.438, f32[32,2,128]{2,1,0:T(2,128)S(1)} %gather_fusion.7, pred[32,128,128]{1,2,0:T(8,128)(4,1)} %fusion.126, bf16[32,2,64,64]{3,2,1,0:T(8,128)(2,1)} %gather_fusion.8, bf16[32,128,2,64]{1,3,2,0:T(8,128)(2,1)} %bitcast.186), kind=kOutput, calls=%fused_computation.21.clone.1 | convolution fusion | flops 206045184 | bytes 8421376 | tf_op jit(solution)/shard_map/while/body/ghij,gjhe->gihe/dot_general | solution.py:123
  323.7 2.9 copy.83
  326.6 4.7 scatter_fusion.2
  331.3 73.8 %pmax.7 = f32[2048,2]{0,1:T(2,128)S(1)} all-reduce(f32[2048,2]{0,1:T(2,128)S(1)} %bitcast.189), channel_id=1, replica_groups=mesh['rel'=4,'node'=2,'head'=4] {'rel'}, use_global_device_ids=true, to_apply=%region_10.11 | all-reduce | flops 4096 | bytes 32768 | tf_op jit(solution)/shard_map/pmax | solution.py:143
  408.8 3.0 reshape.360
  416.6 8.9 %reduce-scatter.10.cloned.1.call-done = bf16[512,2]{1,0:T(8,128)(2,1)} async-done(((bf16[2048,2]{1,0:T(8,128)(2,1)}), bf16[512,2]{1,0:T(8,128)(2,1)}) %reduce-scatter.10.cloned.1.call-update) | async-done | bytes 2064
  426.7 21.0 %reduce-scatter.6.cloned.1.call-done = bf16[512,128]{1,0:T(8,128)(2,1)} async-done(((bf16[2048,128]{1,0:T(8,128)(2,1)}), bf16[512,128]{1,0:T(8,128)(2,1)}) %reduce-scatter.6.cloned.1.call-update) | async-done | bytes 131088 | tf_op jit(solution)/shard_map/reduce_scatter | solution.py:157
  451.2 19.9 %reduce-scatter.8.cloned.1.call-done = bf16[128,512]{1,0:T(8,128)(2,1)} async-done(((bf16[512,512]{1,0:T(8,128)(2,1)}), bf16[128,512]{1,0:T(8,128)(2,1)}) %reduce-scatter.8.cloned.1.call-update) | async-done | bytes 131088 | tf_op jit(solution)/shard_map/reduce_scatter | solution.py:171
  472.1 15.5 %all_gather.11 = bf16[512,512]{1,0:T(8,128)(2,1)S(1)} all-gather(bf16[128,512]{1,0:T(8,128)(2,1)S(1)} %add_convert_fusion), channel_id=1, replica_groups=mesh['rel'=4,'node'=2,'head'=4] {'rel'}, dimensions={0}, use_global_device_ids=true | all-gather | bytes 655360 | tf_op jit(solution)/shard_map/all_gather | solution.py:182
  (213 shorter events, 180.1 us)
Async XLA Ops:
  6.5 16.9 %copy-start = (bf16[64,2,64,64]{3,2,1,0:T(8,128)(2,1)S(1)}, bf16[64,2,64,64]{3,2,1,0:T(8,128)(2,1)}, u32[]{:S(2)}) copy-start(bf16[64,2,64,64]{3,2,1,0:T(8,128)(2,1)} %param.22) | copy-start | bytes 3145732
  6.5 7.1 %copy-start.5 = (bf16[4,512,128]{2,1,0:T(8,128)(2,1)S(1)}, bf16[4,512,128]{2,1,0:T(8,128)(2,1)}, u32[]{:S(2)}) copy-start(bf16[4,512,128]{2,1,0:T(8,128)(2,1)} %param.21) | copy-start | bytes 1572868
  6.5 50.9 %all-gather.3.cloned.1.call-start = ((), (), s32[]{:S(2)}) async-start(), calls=%async_computation.3 | async-start | bytes 1179648 | tf_op jit(solution)/shard_map/all_gather | solution.py:67
  13.6 6.3 %copy-start.1 = (s32[16,1]{0,1:T(1,128)S(1)}, s32[16,1]{0,1:T(1,128)}, u32[]{:S(2)}) copy-start(s32[16,1]{0,1:T(1,128)} %param.31) | copy-start | bytes 196
  13.6 84.9 %all-gather.5.cloned.1.call-start = ((), (), s32[]{:S(2)}) async-start(), calls=%async_computation.4 | async-start | bytes 1179648 | tf_op jit(solution)/shard_map/all_gather | solution.py:68
  15.0 6.8 %copy-start.11 = (s32[16]{0:T(128)S(1)}, s32[16]{0:T(128)}, u32[]{:S(2)}) copy-start(s32[16]{0:T(128)} %param.27) | copy-start | bytes 196
  15.1 8.2 %copy-start.8 = (s32[16,16]{1,0:T(8,128)S(1)}, s32[16,16]{1,0:T(8,128)}, u32[]{:S(2)}) copy-start(s32[16,16]{1,0:T(8,128)} %param.29) | copy-start | bytes 3076
  15.1 8.3 %copy-start.10 = (f32[64,2]{0,1:T(2,128)S(1)}, f32[64,2]{0,1:T(2,128)}, u32[]{:S(2)}) copy-start(f32[64,2]{0,1:T(2,128)} %param.24) | copy-start | bytes 1540
  16.4 9.0 %copy-start.9 = (s32[16,16]{1,0:T(8,128)S(1)}, s32[16,16]{1,0:T(8,128)}, u32[]{:S(2)}) copy-start(s32[16,16]{1,0:T(8,128)} %param.28) | copy-start | bytes 3076
  17.8 13.9 %copy-start.7 = (s32[2048]{0:T(1024)S(1)}, s32[2048]{0:T(1024)}, u32[]{:S(2)}) copy-start(s32[2048]{0:T(1024)} %param.18) | copy-start | bytes 24580
  19.8 405.7 %reduce-scatter.10.cloned.1.call-start = ((), (), s32[]{:S(2)}) async-start(), calls=%async_computation.7 | async-start | bytes 655360
  31.7 2.5 copy-start.2
  34.2 1.7 copy-start.4
  406.3 41.4 %reduce-scatter.6.cloned.1.call-start = ((), (), s32[]{:S(2)}) async-start(), calls=%async_computation.5 | async-start | bytes 655360 | tf_op jit(solution)/shard_map/reduce_scatter | solution.py:157
  407.7 4.1 copy-start.3
  414.1 34.6 %copy-start.6 = (bf16[4,128,512]{2,1,0:T(8,128)(2,1)S(1)}, bf16[4,128,512]{2,1,0:T(8,128)(2,1)}, u32[]{:S(2)}) copy-start(bf16[4,128,512]{2,1,0:T(8,128)(2,1)} %param.25) | copy-start | bytes 1572868
  416.4 54.6 %reduce-scatter.8.cloned.1.call-start = ((), (), s32[]{:S(2)}) async-start(), calls=%async_computation.6 | async-start | bytes 655360 | tf_op jit(solution)/shard_map/reduce_scatter | solution.py:171
  449.3 1.8 copy-start.12
Sparse Core Ops, SparseCore 0:
  13.7 43.6 all-gather.2
  59.5 38.9 all-gather.4
  406.4 19.0 reduce-scatter.9
  427.6 20.0 reduce-scatter.5
  451.1 19.8 reduce-scatter.7
where the time goes:
time: 498 us; the launch traced here: 495 us
  local copies, waits for them, and re-layouts  145 us (29%)
  waiting for transfers between devices  110 us (22%)
  blocking collectives  89.3 us (18%)
  other arithmetic  70.8 us (14%)
  matrix products  64.1 us (13%)
  between operations  14.2 us (3%)
    pmax x1, blocking collectives, per_device(): top = lax.pmax(m_rows, 'rel')  73.8 us
    all_gather x1, waiting for transfers between devices, per_device(): lax.all_gather(values_own, ('rel', 'node'), axis=0, tiled=True)  41.1 us
    dot_general x4, matrix products, visit(): jnp.einsum('ghij,gjhe->gihe', weights.astype(jnp.bfloat16), message, pref...  23 us
    reduce_scatter x1, waiting for transfers between devices, per_device(): lax.psum_scatter(regroup(a_scaled).astype(jnp.bfloat16), 'rel', scatter_d...  21 us
    gather x8, local copies, waits for them, and re-layouts, visit(): k_tiles = key_blocks[src].reshape(group, block, heads, head_size)  20.8 us
    dot_general x16, matrix products, project(): jnp.dot(rows, weights[kind], preferred_element_type=jnp.float32)  20.8 us
    gather x8, local copies, waits for them, and re-layouts, visit(): v_tiles = value_blocks[src].reshape(group, block, heads, head_size)  20.5 us
    dot_general x4, matrix products, visit(): jnp.einsum('gihd,gjhd->ghij', q_tiles, k_tiles, preferred_element_type=jn...  20.4 us
  transfers between devices with their start and end apart: 5, of which 5 were waited for; matrix products, arithmetic and copies ran while one was open for 7% of the time, Pallas kernels for 0%

commit v1 on v0

v1 whole, which is shorter than its diff:
```python
import functools
import math

import jax
import jax.numpy as jnp
from jax import lax
from jax.experimental import pallas as pl
from jax.experimental.pallas import tpu as pltpu
from jax.sharding import PartitionSpec as P

NEG = -1e30
FLOOR = -5e29
LANES = 128
TAIL = 16
GROUP = 4
BF = jnp.bfloat16
F32 = jnp.float32

VMEM = pl.BlockSpec(memory_space=pltpu.VMEM)
SMEM = pl.BlockSpec(memory_space=pltpu.SMEM)
ANY = pl.BlockSpec(memory_space=pl.ANY)


def hits_of(kinds_row, types):
    column = jnp.broadcast_to(kinds_row, (LANES, LANES)).astype(F32).T
    return [jnp.where(column == float(kind), 1.0, 0.0) for kind in range(types)]


def spread(rows, kinds, types):
    wide = rows.shape[1] // LANES
    out = []
    for b in range(rows.shape[0] // LANES):
        block = rows[b * LANES : (b + 1) * LANES]
        parts = []
        for hit in hits_of(kinds[b : b + 1], types):
            parts.append(block * jnp.concatenate([hit.astype(BF)] * wide, axis=1))
        out.append(jnp.concatenate(parts, axis=1))
    return jnp.concatenate(out, axis=0)


def stacked(w_ref):
    types, depth, cols = w_ref.shape
    return w_ref[...].reshape(types * depth, cols)


def kv_body(x_ref, kinds_ref, wk_ref, wv_ref, k_ref, vt_ref):
    types = wk_ref.shape[0]
    cols = wk_ref.shape[2]
    weights = jnp.concatenate([stacked(wk_ref), stacked(wv_ref)], axis=1)
    step = k_ref.shape[0]
    rows = spread(x_ref[...], kinds_ref[0], types)
    both = jnp.dot(rows, weights, preferred_element_type=F32)
    for b in range(step):
        part = both[b * LANES : (b + 1) * LANES]
        k_ref[b] = part[:, :cols].astype(BF)
        vt_ref[b] = part[:, cols:].T.astype(BF)


def q_body(perm_ref, x_ref, kinds_ref, wq_ref, att_ref, msg_ref, qt_ref, attd_ref, msgd_ref, att_s, msg_s, sems):
    types = wq_ref.shape[0]
    positions = attd_ref.shape[0]
    heads, hd = att_ref.shape[1], att_ref.shape[2]
    step = qt_ref.shape[0]

    def copies(p):
        r = perm_ref[p]
        return (
            pltpu.make_async_copy(att_ref.at[r], att_s.at[p], sems.at[0, p]),
            pltpu.make_async_copy(msg_ref.at[r], msg_s.at[p], sems.at[1, p]),
        )

    @pl.when(pl.program_id(0) == 0)
    def _():
        for p in range(positions):
            for copy in copies(p):
                copy.start()

    rows = spread(x_ref[...], kinds_ref[0], types)
    query = jnp.dot(rows, stacked(wq_ref), preferred_element_type=F32)
    for b in range(step):
        qt_ref[b] = query[b * LANES : (b + 1) * LANES].T.astype(BF)

    @pl.when(pl.program_id(0) == pl.num_programs(0) - 1)
    def _():
        for p in range(positions):
            for copy in copies(p):
                copy.wait()
        for p in range(positions):
            for h in range(heads):
                pads = [jnp.zeros((hd, hd), F32)] * heads
                lanes = list(pads)
                lanes[h] = att_s[p, h].astype(F32)
                attd_ref[p, h * hd : (h + 1) * hd, :] = jnp.concatenate(lanes, axis=1).astype(BF)
                lanes = list(pads)
                lanes[h] = msg_s[p, h].astype(F32).T
                msgd_ref[p, h * hd : (h + 1) * hd, :] = jnp.concatenate(lanes, axis=1).astype(BF)


def tiles_body(
    heads, tcap, n_rel, first, last, list_ref, ends_ref, prior_ref, bits_ref, qt_ref, k_ref, vt_ref, attd_ref, msgd_ref, *refs
):
    if first == 0:
        start = 0
    else:
        start = ends_ref[first - 1]
        old_m, old_l, old_a, *refs = refs
    stop = ends_ref[first]
    if last:
        send_ref, m_ref, l_ref, a_ref = refs
    else:
        m_ref, l_ref, a_ref = refs
    cols = qt_ref.shape[1]
    hd = cols // heads
    wide = heads * LANES
    if first == 0:
        m_ref[...] = jnp.full(m_ref.shape, FLOOR, F32)
        l_ref[...] = jnp.zeros(l_ref.shape, F32)
        a_ref[...] = jnp.zeros(a_ref.shape, F32)
    else:
        m_ref[...] = old_m[...]
        l_ref[...] = old_l[...]
        a_ref[...] = old_a[...]
    shift = 31 - lax.broadcasted_iota(jnp.int32, (32, LANES), 0)

    def tile(index):
        code = list_ref[jnp.minimum(index, stop - 1)]
        slot = code & 0xFFF
        src = (code >> 12) & 0xFFF
        dst = code >> 24
        position = lax.div(slot, tcap)
        words = jnp.where(index < stop, bits_ref[slot], 0)
        qrel = jnp.dot(attd_ref[position], qt_ref[dst], preferred_element_type=F32)
        diag = []
        for h in range(heads):
            piece = (qrel[h * hd : (h + 1) * hd] * prior_ref[position * heads + h]).astype(BF)
            row = [jnp.zeros((hd, LANES), BF)] * heads
            row[h] = piece
            diag.append(jnp.concatenate(row, axis=1))
        scores = jnp.dot(k_ref[src], jnp.concatenate(diag, axis=0), preferred_element_type=F32)
        message = jnp.dot(msgd_ref[position], vt_ref[src], preferred_element_type=F32).astype(BF)
        parts = []
        for w in range(words.shape[0]):
            edge = (jnp.broadcast_to(words[w : w + 1], (32, LANES)) << shift) < 0
            for_heads = jnp.concatenate([edge] * heads, axis=1)
            parts.append(jnp.where(for_heads, scores[w * 32 : (w + 1) * 32], NEG))
        masked = jnp.concatenate(parts, axis=0)
        top = jnp.maximum(jnp.max(masked, axis=0, keepdims=True), FLOOR)
        weights = jnp.exp(masked - top)
        total = jnp.sum(weights, axis=0, keepdims=True)
        rounded = weights.astype(BF)
        sums = []
        for h in range(heads):
            sums.append(
                jnp.dot(
                    message[h * hd : (h + 1) * hd],
                    rounded[:, h * LANES : (h + 1) * LANES],
                    preferred_element_type=F32,
                )
            )
        return dst, top, total, sums

    def visit(turn, carry):
        done = [tile(start + turn * GROUP + g) for g in range(GROUP)]
        for dst, top, total, sums in done:
            m_old = m_ref[dst]
            m_new = jnp.maximum(m_old, top)
            keep = jnp.exp(m_old - m_new)
            take = jnp.exp(top - m_new)
            m_ref[dst] = m_new
            l_ref[dst] = l_ref[dst] * keep + total * take
            for h in range(heads):
                lanes = slice(h * LANES, (h + 1) * LANES)
                rows = slice(h * hd, (h + 1) * hd)
                a_ref[dst, rows, :] = a_ref[dst, rows, :] * keep[:, lanes] + sums[h] * take[:, lanes]
        return carry

    lax.fori_loop(0, lax.div(stop - start + GROUP - 1, GROUP), visit, 0)

    if last:
        blocks = a_ref.shape[0]
        n_head = blocks // n_rel
        for b in range(blocks):
            spot = (b % n_rel) * n_head + b // n_rel
            send_ref[spot, :cols, :] = a_ref[b].astype(BF)
            rows = []
            for value, count in ((m_ref[b], 3), (l_ref[b], 3)):
                rest = value
                for _ in range(count):
                    piece = rest.astype(BF).astype(F32)
                    rest = rest - piece
                    rows += [piece[:, h * LANES : (h + 1) * LANES] for h in range(heads)]
            rows.append(jnp.zeros((TAIL - len(rows), LANES), F32))
            send_ref[spot, cols:, :] = jnp.concatenate(rows, axis=0).astype(BF)


def finish_body(heads, n_rel, n_head, me_ref, skip_ref, got_ref, x_ref, kinds_ref, *refs):
    w_refs, out_ref = refs[:-1], refs[-1]
    cols = got_ref.shape[1] - TAIL
    hd = cols // heads
    types = w_refs[0].shape[0]
    hits = hits_of(kinds_ref[...], types)
    hidden = []
    for s in range(n_head):
        h_from = lax.rem(me_ref[0] + n_head - s, n_head)
        accs, tops, totals = [], [], []
        for z in range(n_rel):
            spot = z * n_head + h_from
            accs.append(got_ref[spot, :cols, :])
            tail = got_ref[spot, cols:, :].astype(F32)
            m = tail[0:heads] + tail[heads : 2 * heads] + tail[2 * heads : 3 * heads]
            tail = tail[3 * heads :]
            tops.append(m)
            totals.append(tail[0:heads] + tail[heads : 2 * heads] + tail[2 * heads : 3 * heads])
        top = functools.reduce(jnp.maximum, tops)
        scales = [jnp.exp(m - top) for m in tops]
        total = functools.reduce(jnp.add, [l * e for l, e in zip(totals, scales)])
        inverse = 1.0 / jnp.maximum(total, 1.0)
        rows = []
        for h in range(heads):
            acc = functools.reduce(
                jnp.add,
                [a[h * hd : (h + 1) * hd].astype(F32) * e[h : h + 1] for a, e in zip(accs, scales)],
            )
            rows.append(jax.nn.gelu(acc * inverse[h : h + 1]))
        hidden.append(jnp.concatenate(rows, axis=0).T.astype(BF))
    mixed = None
    for s in range(n_head):
        w = w_refs[s][...].reshape(types * cols, -1)
        spread_rows = jnp.concatenate([hidden[s] * hit.astype(BF) for hit in hits], axis=1)
        part = jnp.dot(spread_rows, w, preferred_element_type=F32)
        mixed = part if mixed is None else mixed + part
    gate = jnp.zeros((LANES, LANES), F32)
    for kind in range(types):
        gate = gate + hits[kind] * jax.nn.sigmoid(jnp.full((LANES, LANES), skip_ref[kind], F32))
    gate = jnp.concatenate([gate] * (mixed.shape[1] // LANES), axis=1)
    out_ref[...] = (gate * mixed + (1.0 - gate) * x_ref[...].astype(F32)).astype(BF)


def shifted(n, s):
    return [(i, (i + s) % n) for i in range(n)]


def listed(tile_src, tile_dst, tile_count, blocks, me, n_node):
    positions, tcap = tile_src.shape
    slots = positions * tcap
    src = tile_src.reshape(slots)
    dst = tile_dst.reshape(slots)
    ids = jnp.arange(slots, dtype=jnp.int32)
    live = (jnp.arange(tcap, dtype=jnp.int32)[None, :] < tile_count).reshape(slots)
    away = (me - src // blocks) % n_node
    near = live & (away == 0)
    far = live & (away != 0)
    place = src % blocks + jnp.maximum(away - 1, 0) * blocks
    code = ids | (place << 12) | (dst << 24)
    n_near = jnp.sum(near.astype(jnp.int32))
    n_live = jnp.sum(live.astype(jnp.int32))
    before = ids[None, :] < ids[:, None]
    near_rank = jnp.sum((before & near[None, :]).astype(jnp.int32), axis=1)
    far_rank = jnp.sum((before & far[None, :]).astype(jnp.int32), axis=1)
    rank = jnp.where(near, near_rank, jnp.where(far, n_near + far_rank, -1))
    order = jnp.sum(jnp.where(rank[None, :] == ids[:, None], code[None, :], 0), axis=1)
    return order, jnp.stack([n_near, n_live])


def per_device(
    features,
    node_type,
    w_query,
    w_key,
    w_value,
    rel_att,
    rel_msg,
    rel_prior,
    w_out,
    skip,
    rel_perm,
    tile_src,
    tile_dst,
    tile_bits,
    tile_count,
):
    node_rows, depth = features.shape
    n_rel = lax.axis_size("rel")
    n_node = lax.axis_size("node")
    n_head = lax.axis_size("head")
    heads = rel_prior.shape[1]
    types, _, cols = w_query.shape
    hd = cols // heads
    positions, tcap, block, words = tile_bits.shape
    blocks = node_rows // block
    slots = positions * tcap
    kinds = node_type.reshape(blocks, block)

    w_parts = [w_out] + [lax.ppermute(w_out, "head", shifted(n_head, s)) for s in range(1, n_head)]

    step = math.gcd(4, blocks)
    x_spec = pl.BlockSpec((step * block, depth), lambda i: (i, 0))
    kinds_spec = pl.BlockSpec((1, step, block), lambda i: (i, 0, 0))
    w_spec = pl.BlockSpec((types, depth, cols), lambda i: (0, 0, 0))
    b_spec = pl.BlockSpec((step, block, cols), lambda i: (i, 0, 0))
    bt_spec = pl.BlockSpec((step, cols, block), lambda i: (i, 0, 0))
    kinds_in = kinds.reshape(blocks // step, step, block)
    keys, values_t = pl.pallas_call(
        kv_body,
        grid=(blocks // step,),
        in_specs=[x_spec, kinds_spec, w_spec, w_spec],
        out_specs=[b_spec, bt_spec],
        out_shape=[
            jax.ShapeDtypeStruct((blocks, block, cols), BF),
            jax.ShapeDtypeStruct((blocks, cols, block), BF),
        ],
        name="keys_values",
    )(features, kinds_in, w_key, w_value)

    far_keys = [lax.ppermute(keys, "node", shifted(n_node, s)) for s in range(1, n_node)]
    far_values = [lax.ppermute(values_t, "node", shifted(n_node, s)) for s in range(1, n_node)]

    d_spec = pl.BlockSpec((positions, cols, cols), lambda i, perm: (0, 0, 0))
    queries_t, att_d, msg_d = pl.pallas_call(
        q_body,
        grid_spec=pltpu.PrefetchScalarGridSpec(
            num_scalar_prefetch=1,
            grid=(blocks // step,),
            in_specs=[
                pl.BlockSpec((step * block, depth), lambda i, perm: (i, 0)),
                pl.BlockSpec((1, step, block), lambda i, perm: (i, 0, 0)),
                pl.BlockSpec((types, depth, cols), lambda i, perm: (0, 0, 0)),
                ANY,
                ANY,
            ],
            out_specs=[pl.BlockSpec((step, cols, block), lambda i, perm: (i, 0, 0)), d_spec, d_spec],
            scratch_shapes=[
                pltpu.VMEM((positions, heads, hd, hd), BF),
                pltpu.VMEM((positions, heads, hd, hd), BF),
                pltpu.SemaphoreType.DMA((2, positions)),
            ],
        ),
        out_shape=[
            jax.ShapeDtypeStruct((blocks, cols, block), BF),
            jax.ShapeDtypeStruct((positions, cols, cols), BF),
            jax.ShapeDtypeStruct((positions, cols, cols), BF),
        ],
        name="queries",
    )(rel_perm, features, kinds_in, w_query, rel_att, rel_msg)

    order, ends = listed(tile_src, tile_dst, tile_count, blocks, lax.axis_index("node"), n_node)
    prior = (rel_prior[rel_perm] * (1.0 / math.sqrt(hd))).reshape(positions * heads)
    bits = tile_bits.transpose(0, 1, 3, 2).reshape(slots, words, block)
    state_shapes = [
        jax.ShapeDtypeStruct((blocks, 1, heads * block), F32),
        jax.ShapeDtypeStruct((blocks, 1, heads * block), F32),
        jax.ShapeDtypeStruct((blocks, cols, block), F32),
    ]
    state = pl.pallas_call(
        functools.partial(tiles_body, heads, tcap, n_rel, 0, False),
        in_specs=[SMEM, SMEM, SMEM] + [VMEM] * 6,
        out_specs=[VMEM] * 3,
        out_shape=state_shapes,
        name="near_tiles",
    )(order, ends, prior, bits, queries_t, keys, values_t, att_d, msg_d)

    def joined(arrays):
        return arrays[0] if len(arrays) == 1 else jnp.concatenate(arrays, axis=0)

    send = pl.pallas_call(
        functools.partial(tiles_body, heads, tcap, n_rel, 1, True),
        in_specs=[SMEM, SMEM, SMEM] + [VMEM] * 9,
        out_specs=VMEM,
        out_shape=jax.ShapeDtypeStruct((blocks, cols + TAIL, block), BF),
        scratch_shapes=[pltpu.VMEM(s.shape, s.dtype) for s in state_shapes],
        name="far_tiles",
    )(order, ends, prior, bits, queries_t, joined(far_keys), joined(far_values), att_d, msg_d, *state)

    got = lax.all_to_all(send, ("rel", "head"), 0, 0, tiled=True)

    spot = lax.axis_index("head") * n_rel + lax.axis_index("rel")
    own_rows = lax.dynamic_slice_in_dim(features, spot * block, block, 0)
    own_kinds = lax.dynamic_slice_in_dim(kinds, spot, 1, 0)
    finished = pl.pallas_call(
        functools.partial(finish_body, heads, n_rel, n_head),
        in_specs=[SMEM, SMEM] + [VMEM] * (3 + n_head),
        out_specs=VMEM,
        out_shape=jax.ShapeDtypeStruct((block, depth), BF),
        name="finish",
    )(lax.axis_index("head").reshape(1), skip, got, own_rows, own_kinds, *w_parts)
    return lax.all_gather(finished, "rel", axis=0, tiled=True)


def solution(mesh):
    in_specs = (
        P("node", None),
        P("node"),
        P(None, None, "head"),
        P(None, None, "head"),
        P(None, None, "head"),
        P(None, "head", None, None),
        P(None, "head", None, None),
        P(None, "head"),
        P(None, "head", None),
        P(),
        P("rel"),
        P("rel", "node"),
        P("rel", "node"),
        P("rel", "node", None, None),
        P("rel", "node"),
    )
    out_specs = P(("node", "head"), None)
    return jax.shard_map(
        per_device, mesh=mesh, in_specs=in_specs, out_specs=out_specs, check_vma=False
    )
```

time: 498 us -> 136 us (0.27)
  local copies, waits for them, and re-layouts: 145 us -> 7.15 us
  waiting for transfers between devices: 110 us -> 23.4 us
  Pallas kernels: 0 us -> 73.2 us
  blocking collectives: 89.3 us -> 16.8 us
  other arithmetic: 70.8 us -> 4.19 us
  matrix products: 64.1 us -> 0 us
  between operations: 14.2 us -> 0.14 us
  starting transfers between devices: 0.17 us -> 10 us
    gather x56 -> x1, local copies, waits for them, and re-layouts: 108 us -> 0.56 us  [per_device(): rel_prior[rel_perm] * (1.0 / math.sqrt(hd))]
    pmax x1 -> x0, blocking collectives: 73.8 us -> none  [per_device(): top = lax.pmax(m_rows, 'rel')]
    pallas_call x0 -> x5, Pallas kernels: none -> 73.2 us  [the longest x1 29.7 us: per_device(): pl.pallas_call(functools.partial(tiles_body, heads, tcap, n_rel, 0, False...]
    dot_general x24 -> x0, matrix products: 64.1 us -> none  [the longest x4 23 us: visit(): jnp.einsum('ghij,gjhe->gihe', weights.astype(jnp.bfloat16), message, pref...]
    all_gather x2 -> x0, waiting for transfers between devices: 60.4 us -> none  [the longest x1 41.1 us: per_device(): lax.all_gather(values_own, ('rel', 'node'), axis=0, tiled=True)]
    reduce_scatter x2 -> x0, waiting for transfers between devices: 40.9 us -> none  [the longest x1 21 us: per_device(): lax.psum_scatter(regroup(a_scaled).astype(jnp.bfloat16), 'rel', scatter_d...]
    scatter-add x8 -> x0, other arithmetic: 25.3 us -> none  [the longest x4 18.6 us: visit(): acc_new = (acc * spread).at[dst].add(weighted)]
    reshape x12 -> x1, local copies, waits for them, and re-layouts: 25.4 us -> 0.08 us  [listed(): src = tile_src.reshape(slots)]
  transfers between devices with their start and end apart: 5 -> 6, of which waited for: 5 -> 3; matrix products, arithmetic and copies ran while one was open for 7% -> 6% of each run, Pallas kernels for 0% -> 28%
where the time goes in v1:
time: 136 us; the launch traced here: 135 us
  Pallas kernels  73.2 us (54%)
  waiting for transfers between devices  23.4 us (17%)
  blocking collectives  16.8 us (12%)
  starting transfers between devices  10 us (7%)
  local copies, waits for them, and re-layouts  7.15 us (5%)
  other arithmetic  4.19 us (3%)
    pallas_call x1, Pallas kernels, per_device(): pl.pallas_call(functools.partial(tiles_body, heads, tcap, n_rel, 0, False...  29.7 us
    pallas_call x1, Pallas kernels, per_device(): pl.pallas_call(functools.partial(tiles_body, heads, tcap, n_rel, 1, True)...  27.2 us
    ppermute x3, waiting for transfers between devices, per_device(): lax.ppermute(w_out, 'head', shifted(n_head, s))  23.4 us
    all_gather x1, blocking collectives, per_device(): return lax.all_gather(finished, 'rel', axis=0, tiled=True)  16.8 us
    pallas_call x1, Pallas kernels, per_device(): pl.pallas_call(q_body, grid_spec=pltpu.PrefetchScalarGridSpec(num_scalar_...  7.44 us
    pallas_call x1, Pallas kernels, per_device(): pl.pallas_call(kv_body, grid=(blocks // step,), in_specs=[x_spec, kinds_s...  5.75 us
    all_to_all x1, starting transfers between devices, per_device(): got = lax.all_to_all(send, ('rel', 'head'), 0, 0, tiled=True)  3.58 us
    ppermute x3, starting transfers between devices, per_device(): lax.ppermute(w_out, 'head', shifted(n_head, s))  3.4 us
  transfers between devices with their start and end apart: 6, of which 3 were waited for; matrix products, arithmetic and copies ran while one was open for 6% of the time, Pallas kernels for 28%

profile of v1, /device:TPU:0, one launch (start us, length us, event | category | flops | bytes accessed | tf_op | source)
XLA Modules:
  0.0 134.8 jit_solution(11443852250388390765)
XLA Ops:
  0.0 5.8 %keys_values.1 = (bf16[16,128,128]{2,1,0:T(8,128)(2,1)}, bf16[16,128,128]{2,1,0:T(8,128)(2,1)}) custom-call(bf16[2048,512]{1,0:T(8,128)(2,1)} %x_ref.3, s32[4,4,128]{2,1,0:T(4,128)} %bitcast.11, bf16[4,512,128]{2,1,0:T(8,128)(2,1)} %wk_ref.1, bf16[4,512,128]{2,1,0:T(8,128)(2,1)} %wv_ref.1), custom_call_target="tpu_custom_call" | custom-call | tf_op jit(solution)/shard_map/keys_values/pallas_call | solution.py:303
  5.8 3.0 %collective-permute-start = (bf16[16,128,128]{2,1,0:T(8,128)(2,1)}, bf16[16,128,128]{2,1,0:T(8,128)(2,1)S(1)}, u32[]{:S(2)}, u32[]{:S(2)}) collective-permute-start(bf16[16,128,128]{2,1,0:T(8,128)(2,1)} %get-tuple-element.14.k_ref), channel_id=1, source_target_pairs={{0,4},{4,0},{1,5},{5,1},{2,6},{6,2},{3,7},{7,3},{8,12},{12,8},{9,1... | collective-permute-start | bytes 1572872 | tf_op jit(solution)/shard_map/ppermute | solution.py:315
  8.9 0.1 lt.77
  9.0 0.1 reshape.158
  9.1 0.7 convert_reduce_fusion.2
  9.8 0.1 convert_reduce_fusion.1
  10.0 0.1 copy.18
  10.2 0.6 gather_fusion
  10.7 0.6 mul.27.prior_ref
  11.4 7.4 %queries.1 = (bf16[16,128,128]{2,1,0:T(8,128)(2,1)}, bf16[16,128,128]{2,1,0:T(8,128)(2,1)}, bf16[16,128,128]{2,1,0:T(8,128)(2,1)}) custom-call(s32[16]{0:T(128)} %perm_ref.1, bf16[2048,512]{1,0:T(8,128)(2,1)} %x_ref.3, s32[4,4,128]{2,1,0:T(4,128)} %bitcast.12, bf16[4,512,128]{2,1,0:T(8,128)(2,1)} %wq_ref.1, bf16[64,2,64,64]{3,2,1,0:T(8,128)(2,1)} %att_ref.1, ...), custom_call_target="tpu_custom_call" | custom-call | tf_op jit(solution)/shard_map/queries/pallas_call | solution.py:319
  18.8 1.8 %pad_add_fusion.ends_ref = s32[2]{0:T(128)} fusion(s32[1]{0:T(128)} %bitcast.3, s32[1]{0:T(128)} %bitcast.2), kind=kLoop, calls=%fused_computation.43 | loop fusion | flops 2 | bytes 16 | tf_op jit(solution)/shard_map/stack | solution.py:262
  20.6 0.1 convert_reduce_fusion
  20.7 0.6 or_or_fusion
  21.4 0.7 select_reduce_fusion.list_ref
  22.0 29.7 %near_tiles.1 = (f32[16,1,256]{2,1,0:T(1,128)}, f32[16,1,256]{2,1,0:T(1,128)}, f32[16,128,128]{2,1,0:T(8,128)}) custom-call(s32[256]{0:T(256)} %select_reduce_fusion.list_ref, s32[2]{0:T(128)} %pad_add_fusion.ends_ref, f32[32]{0:T(128)} %mul.27.prior_ref, s32[256,4,128]{2,1,0:T(4,128)} %bitcast.9, bf16[16,128,128]{2,1,0:T(8,128)(2,1)} %get-tuple-element.13.qt_ref, ...), custom_call_target="tpu_custom_call" | custom-call | tf_op jit(solution)/shard_map/near_tiles/pallas_call | solution.py:354
  51.7 0.8 copy-done.1
  52.5 0.2 copy-done.2
  52.7 27.2 %far_tiles.1 = bf16[16,144,128]{2,1,0:T(8,128)(2,1)} custom-call(s32[256]{0:T(256)} %select_reduce_fusion.list_ref, s32[2]{0:T(128)} %pad_add_fusion.ends_ref, f32[32]{0:T(128)} %mul.27.prior_ref, s32[256,4,128]{2,1,0:T(4,128)} %bitcast.10, bf16[16,128,128]{2,1,0:T(8,128)(2,1)} %get-tuple-element.13.qt_ref, bf16[16,128,128]{2,1,0:T(8,128)(2,1)} %copy-done.1, ...), custom_call_target="tpu_custom_call" | custom-call | tf_op jit(solution)/shard_map/far_tiles/pallas_call | solution.py:365
  79.9 3.6 %all-to-all-start = ((bf16[16,144,128]{2,1,0:T(8,128)(2,1)}), bf16[16,144,128]{2,1,0:T(8,128)(2,1)S(1)}, u32[]{:S(2)}, u32[]{:S(2)}) async-start(bf16[16,144,128]{2,1,0:T(8,128)(2,1)} %far_tiles.1), calls=%async_computation | async-start | bytes 1179648 | tf_op jit(solution)/shard_map/all_to_all | solution.py:374
  83.5 0.3 collective-permute-start.2
  83.8 1.7 %collective-permute-start.3 = (bf16[4,128,512]{2,1,0:T(8,128)(2,1)S(1)}, bf16[4,128,512]{2,1,0:T(8,128)(2,1)S(1)}, u32[]{:S(2)}, u32[]{:S(2)}) collective-permute-start(bf16[4,128,512]{2,1,0:T(8,128)(2,1)S(1)} %copy-done.3), channel_id=1, source_target_pairs={{0,2},{1,3},{2,0},{3,1},{4,6},{5,7},{6,4},{7,5},{8,10},{9,11},{10,... | collective-permute-start | bytes 1572872 | tf_op jit(solution)/shard_map/ppermute | solution.py:294
  85.5 1.4 %collective-permute-start.4 = (bf16[4,128,512]{2,1,0:T(8,128)(2,1)S(1)}, bf16[4,128,512]{2,1,0:T(8,128)(2,1)S(1)}, u32[]{:S(2)}, u32[]{:S(2)}) collective-permute-start(bf16[4,128,512]{2,1,0:T(8,128)(2,1)S(1)} %copy-done.3), channel_id=1, source_target_pairs={{0,3},{1,0},{2,1},{3,2},{4,7},{5,4},{6,5},{7,6},{8,11},{9,8},{10,9... | collective-permute-start | bytes 1572872 | tf_op jit(solution)/shard_map/ppermute | solution.py:294
  86.9 1.3 constant_dynamic-slice_fusion.1.kinds_ref
  88.1 1.6 %constant_dynamic-slice_fusion.x_ref = bf16[128,512]{1,0:T(8,128)(2,1)} fusion(bf16[2048,512]{1,0:T(8,128)(2,1)} %x_ref.3, s32[]{:T(128)S(6)} %select_n.89), kind=kLoop, calls=%fused_computation.46 | loop fusion | bytes 262148 | tf_op jit(solution)/shard_map/dynamic_slice | solution.py:377
  89.7 13.7 %collective-permute-done.2.refs_1_ = bf16[4,128,512]{2,1,0:T(8,128)(2,1)S(1)} collective-permute-done((bf16[4,128,512]{2,1,0:T(8,128)(2,1)S(1)}, bf16[4,128,512]{2,1,0:T(8,128)(2,1)S(1)}, u32[]{:S(2)}, u32[]{:S(2)}) %collective-permute-start.2) | collective-permute-done | bytes 524320 | tf_op jit(solution)/shard_map/ppermute | solution.py:294
  103.4 1.1 collective-permute-done.3.refs_2_
  104.6 8.6 %collective-permute-done.4.refs_3_ = bf16[4,128,512]{2,1,0:T(8,128)(2,1)S(1)} collective-permute-done((bf16[4,128,512]{2,1,0:T(8,128)(2,1)S(1)}, bf16[4,128,512]{2,1,0:T(8,128)(2,1)S(1)}, u32[]{:S(2)}, u32[]{:S(2)}) %collective-permute-start.4) | collective-permute-done | bytes 524320 | tf_op jit(solution)/shard_map/ppermute | solution.py:294
  113.2 0.8 copy-done.6
  113.9 0.2 copy-done
  114.2 3.1 %finish.1 = bf16[128,512]{1,0:T(8,128)(2,1)} custom-call(s32[1]{0:T(128)} %bitcast.me_ref, f32[4]{0:T(128)} %skip_ref.1, bf16[16,144,128]{2,1,0:T(8,128)(2,1)} %copy-done, bf16[128,512]{1,0:T(8,128)(2,1)} %constant_dynamic-slice_fusion.x_ref, s32[1,128]{1,0:T(1,128)} %constant_dynamic-slice_fusion.1.kinds_ref, bf16[4,128,512]{2,1,0:T(8,128)(2,1)} %refs_0_.1, ...), custom_call_target="tpu_custom_call" | custom-call | tf_op jit(solution)/shard_map/finish/pallas_call | solution.py:379
  117.3 16.8 %all_gather.3 = bf16[512,512]{1,0:T(8,128)(2,1)S(1)} all-gather(bf16[128,512]{1,0:T(8,128)(2,1)} %finish.1), channel_id=1, replica_groups=mesh['rel'=4,'node'=2,'head'=4] {'rel'}, dimensions={0}, use_global_device_ids=true | all-gather | bytes 655360 | tf_op jit(solution)/shard_map/all_gather | solution.py:386
  134.0 0.8 copy.20
  (32 shorter events, 0.3 us)
Async XLA Ops:
  0.0 8.8 %copy-start.9 = (s32[16,1]{0,1:T(1,128)S(1)}, s32[16,1]{0,1:T(1,128)}, u32[]{:S(2)}) copy-start(s32[16,1]{0,1:T(1,128)} %param.29) | copy-start | bytes 196
  0.0 9.0 %copy-start.7 = (s32[16,16]{1,0:T(8,128)S(1)}, s32[16,16]{1,0:T(8,128)}, u32[]{:S(2)}) copy-start(s32[16,16]{1,0:T(8,128)} %param.26) | copy-start | bytes 3076
  0.0 9.9 %copy-start.8 = (s32[16,16]{1,0:T(8,128)S(1)}, s32[16,16]{1,0:T(8,128)}, u32[]{:S(2)}) copy-start(s32[16,16]{1,0:T(8,128)} %param.27) | copy-start | bytes 3076
  0.0 10.0 %copy-start.10 = (f32[64,2]{0,1:T(2,128)S(1)}, f32[64,2]{0,1:T(2,128)}, u32[]{:S(2)}) copy-start(f32[64,2]{0,1:T(2,128)} %param.22) | copy-start | bytes 1540
  0.0 10.1 %copy-start.11 = (s32[16]{0:T(128)S(1)}, s32[16]{0:T(128)}, u32[]{:S(2)}) copy-start(s32[16]{0:T(128)} %perm_ref.1) | copy-start | bytes 196
  5.8 45.9 %collective-permute-start = (bf16[16,128,128]{2,1,0:T(8,128)(2,1)}, bf16[16,128,128]{2,1,0:T(8,128)(2,1)S(1)}, u32[]{:S(2)}, u32[]{:S(2)}) collective-permute-start(bf16[16,128,128]{2,1,0:T(8,128)(2,1)} %get-tuple-element.14.k_ref), channel_id=1, source_target_pairs={{0,4},{4,0},{1,5},{5,1},{2,6},{6,2},{3,7},{7,3},{8,12},{12,8},{9,1... | collective-permute-start | bytes 1572872 | tf_op jit(solution)/shard_map/ppermute | solution.py:315
  8.7 43.0 %collective-permute-start.1 = (bf16[16,128,128]{2,1,0:T(8,128)(2,1)}, bf16[16,128,128]{2,1,0:T(8,128)(2,1)S(1)}, u32[]{:S(2)}, u32[]{:S(2)}) collective-permute-start(bf16[16,128,128]{2,1,0:T(8,128)(2,1)} %get-tuple-element.15.vt_ref), channel_id=1, source_target_pairs={{0,4},{4,0},{1,5},{5,1},{2,6},{6,2},{3,7},{7,3},{8,12},{12,8},{9,1... | collective-permute-start | bytes 1572872 | tf_op jit(solution)/shard_map/ppermute | solution.py:316
  51.7 0.8 copy-start.1
  51.7 1.0 copy-start.2
  52.7 30.8 %copy-start.3 = (bf16[4,128,512]{2,1,0:T(8,128)(2,1)S(1)}, bf16[4,128,512]{2,1,0:T(8,128)(2,1)}, u32[]{:S(2)}) copy-start(bf16[4,128,512]{2,1,0:T(8,128)(2,1)} %refs_0_.1) | copy-start | bytes 1572868
  79.9 33.3 %all-to-all-start = ((bf16[16,144,128]{2,1,0:T(8,128)(2,1)}), bf16[16,144,128]{2,1,0:T(8,128)(2,1)S(1)}, u32[]{:S(2)}, u32[]{:S(2)}) async-start(bf16[16,144,128]{2,1,0:T(8,128)(2,1)} %far_tiles.1), calls=%async_computation | async-start | bytes 1179648 | tf_op jit(solution)/shard_map/all_to_all | solution.py:374
  83.5 20.0 %collective-permute-start.2 = (bf16[4,128,512]{2,1,0:T(8,128)(2,1)S(1)}, bf16[4,128,512]{2,1,0:T(8,128)(2,1)S(1)}, u32[]{:S(2)}, u32[]{:S(2)}) collective-permute-start(bf16[4,128,512]{2,1,0:T(8,128)(2,1)S(1)} %copy-done.3), channel_id=1, source_target_pairs={{0,1},{1,2},{2,3},{3,0},{4,5},{5,6},{6,7},{7,4},{8,9},{9,10},{10,1... | collective-permute-start | bytes 1572872 | tf_op jit(solution)/shard_map/ppermute | solution.py:294
  83.8 20.8 %collective-permute-start.3 = (bf16[4,128,512]{2,1,0:T(8,128)(2,1)S(1)}, bf16[4,128,512]{2,1,0:T(8,128)(2,1)S(1)}, u32[]{:S(2)}, u32[]{:S(2)}) collective-permute-start(bf16[4,128,512]{2,1,0:T(8,128)(2,1)S(1)} %copy-done.3), channel_id=1, source_target_pairs={{0,2},{1,3},{2,0},{3,1},{4,6},{5,7},{6,4},{7,5},{8,10},{9,11},{10,... | collective-permute-start | bytes 1572872 | tf_op jit(solution)/shard_map/ppermute | solution.py:294
  85.5 27.7 %collective-permute-start.4 = (bf16[4,128,512]{2,1,0:T(8,128)(2,1)S(1)}, bf16[4,128,512]{2,1,0:T(8,128)(2,1)S(1)}, u32[]{:S(2)}, u32[]{:S(2)}) collective-permute-start(bf16[4,128,512]{2,1,0:T(8,128)(2,1)S(1)} %copy-done.3), channel_id=1, source_target_pairs={{0,3},{1,0},{2,1},{3,2},{4,7},{5,4},{6,5},{7,6},{8,11},{9,8},{10,9... | collective-permute-start | bytes 1572872 | tf_op jit(solution)/shard_map/ppermute | solution.py:294
  103.4 9.7 %copy-start.4 = (bf16[4,128,512]{2,1,0:T(8,128)(2,1)}, bf16[4,128,512]{2,1,0:T(8,128)(2,1)S(1)}, u32[]{:S(2)}) copy-start(bf16[4,128,512]{2,1,0:T(8,128)(2,1)S(1)} %collective-permute-done.2.refs_1_) | copy-start | bytes 1572868
  104.6 8.6 %copy-start.5 = (bf16[4,128,512]{2,1,0:T(8,128)(2,1)}, bf16[4,128,512]{2,1,0:T(8,128)(2,1)S(1)}, u32[]{:S(2)}) copy-start(bf16[4,128,512]{2,1,0:T(8,128)(2,1)S(1)} %collective-permute-done.3.refs_2_) | copy-start | bytes 1572868
  113.1 0.8 copy-start.6
  113.1 1.0 copy-start

commit v2 on v1

--- a/solution.py
+++ b/solution.py
@@ -7,6 +7,7 @@
 from jax.experimental import pallas as pl
 from jax.experimental.pallas import tpu as pltpu
 from jax.sharding import PartitionSpec as P
+
 
 NEG = -1e30
 FLOOR = -5e29
@@ -105,13 +106,13 @@
         start = ends_ref[first - 1]
         old_m, old_l, old_a, *refs = refs
     stop = ends_ref[first]
+    *refs, q_s, w_s, v_s, t_s = refs
     if last:
         send_ref, m_ref, l_ref, a_ref = refs
     else:
         m_ref, l_ref, a_ref = refs
     cols = qt_ref.shape[1]
     hd = cols // heads
-    wide = heads * LANES
     if first == 0:
         m_ref[...] = jnp.full(m_ref.shape, FLOOR, F32)
         l_ref[...] = jnp.zeros(l_ref.shape, F32)
@@ -120,48 +121,42 @@
         m_ref[...] = old_m[...]
         l_ref[...] = old_l[...]
         a_ref[...] = old_a[...]
+    q_s[...] = jnp.zeros(q_s.shape, BF)
+    w_s[...] = jnp.zeros(w_s.shape, BF)
+    v_s[...] = jnp.zeros(v_s.shape, BF)
+    t_s[0] = jnp.full(t_s.shape[1:], FLOOR, F32)
+    t_s[1] = jnp.zeros(t_s.shape[1:], F32)
     shift = 31 - lax.broadcasted_iota(jnp.int32, (32, LANES), 0)
 
-    def tile(index):
-        code = list_ref[jnp.minimum(index, stop - 1)]
+    def read(index):
+        code = list_ref[jnp.clip(index, start, stop - 1)]
         slot = code & 0xFFF
-        src = (code >> 12) & 0xFFF
-        dst = code >> 24
-        position = lax.div(slot, tcap)
-        words = jnp.where(index < stop, bits_ref[slot], 0)
-        qrel = jnp.dot(attd_ref[position], qt_ref[dst], preferred_element_type=F32)
-        diag = []
-        for h in range(heads):
-            piece = (qrel[h * hd : (h + 1) * hd] * prior_ref[position * heads + h]).astype(BF)
-            row = [jnp.zeros((hd, LANES), BF)] * heads
-            row[h] = piece
-            diag.append(jnp.concatenate(row, axis=1))
-        scores = jnp.dot(k_ref[src], jnp.concatenate(diag, axis=0), preferred_element_type=F32)
-        message = jnp.dot(msgd_ref[position], vt_ref[src], preferred_element_type=F32).astype(BF)
-        parts = []
-        for w in range(words.shape[0]):
-            edge = (jnp.broadcast_to(words[w : w + 1], (32, LANES)) << shift) < 0
-            for_heads = jnp.concatenate([edge] * heads, axis=1)
-            parts.append(jnp.where(for_heads, scores[w * 32 : (w + 1) * 32], NEG))
-        masked = jnp.concatenate(parts, axis=0)
-        top = jnp.maximum(jnp.max(masked, axis=0, keepdims=True), FLOOR)
-        weights = jnp.exp(masked - top)
-        total = jnp.sum(weights, axis=0, keepdims=True)
-        rounded = weights.astype(BF)
-        sums = []
-        for h in range(heads):
+        return slot, (code >> 12) & 0xFFF, code >> 24, lax.div(slot, tcap)
+
+    def visit(turn, carry):
+        base = start + turn * GROUP
+        sums, scores, messages, queries = [], [], [], []
+        for g in range(GROUP):
             sums.append(
-                jnp.dot(
-                    message[h * hd : (h + 1) * hd],
-                    rounded[:, h * LANES : (h + 1) * LANES],
-                    preferred_element_type=F32,
-                )
+                [
+                    jnp.dot(
+                        v_s[g, h * hd : (h + 1) * hd, :],
+                        w_s[g, :, h * LANES : (h + 1) * LANES],
+                        preferred_element_type=F32,
+                    )
+                    for h in range(heads)
+                ]
             )
-        return dst, top, total, sums
-
-    def visit(turn, carry):
-        done = [tile(start + turn * GROUP + g) for g in range(GROUP)]
-        for dst, top, total, sums in done:
+        for g in range(GROUP):
+            slot, src, dst, position = read(base - GROUP + g)
+            scores.append(jnp.dot(k_ref[src], q_s[g], preferred_element_type=F32))
+            messages.append(jnp.dot(msgd_ref[position], vt_ref[src], preferred_element_type=F32))
+        for g in range(GROUP):
+            slot, src, dst, position = read(base + g)
+            queries.append(jnp.dot(attd_ref[position], qt_ref[dst], preferred_element_type=F32))
+        for g in range(GROUP):
+            slot, src, dst, position = read(base - 2 * GROUP + g)
+            top, total = t_s[0, g], t_s[1, g]
             m_old = m_ref[dst]
             m_new = jnp.maximum(m_old, top)
             keep = jnp.exp(m_old - m_new)
@@ -171,10 +166,34 @@
             for h in range(heads):
                 lanes = slice(h * LANES, (h + 1) * LANES)
                 rows = slice(h * hd, (h + 1) * hd)
-                a_ref[dst, rows, :] = a_ref[dst, rows, :] * keep[:, lanes] + sums[h] * take[:, lanes]
+                a_ref[dst, rows, :] = a_ref[dst, rows, :] * keep[:, lanes] + sums[g][h] * take[:, lanes]
+        for g in range(GROUP):
+            index = base - GROUP + g
+            slot, src, dst, position = read(index)
+            valid = jnp.logical_and(index >= start, index < stop)
+            words = jnp.where(valid, bits_ref[slot], 0)
+            parts = []
+            for w in range(words.shape[0]):
+                edge = (jnp.broadcast_to(words[w : w + 1], (32, LANES)) << shift) < 0
+                for_heads = jnp.concatenate([edge] * heads, axis=1)
+                parts.append(jnp.where(for_heads, scores[g][w * 32 : (w + 1) * 32], NEG))
+            masked = jnp.concatenate(parts, axis=0)
+            top = jnp.maximum(jnp.max(masked, axis=0, keepdims=True), FLOOR)
+            weights = jnp.exp(masked - top)
+            t_s[0, g] = top
+            t_s[1, g] = jnp.sum(weights, axis=0, keepdims=True)
+            w_s[g] = weights.astype(BF)
+            v_s[g] = messages[g].astype(BF)
+        for g in range(GROUP):
+            slot, src, dst, position = read(base + g)
+            for h in range(heads):
+                rows = slice(h * hd, (h + 1) * hd)
+                piece = queries[g][rows] * prior_ref[position * heads + h]
+                q_s[g, rows, h * LANES : (h + 1) * LANES] = piece.astype(BF)
         return carry
 
-    lax.fori_loop(0, lax.div(stop - start + GROUP - 1, GROUP), visit, 0)
+    count = stop - start
+    lax.fori_loop(0, jnp.where(count > 0, lax.div(count + GROUP - 1, GROUP) + 2, 0), visit, 0)
 
     if last:
         blocks = a_ref.shape[0]
@@ -262,7 +281,7 @@
     return order, jnp.stack([n_near, n_live])
 
 
-def per_device(
+def layer(
     features,
     node_type,
     w_query,
@@ -351,11 +370,18 @@
         jax.ShapeDtypeStruct((blocks, 1, heads * block), F32),
         jax.ShapeDtypeStruct((blocks, cols, block), F32),
     ]
+    stage = [
+        pltpu.VMEM((GROUP, cols, heads * block), BF),
+        pltpu.VMEM((GROUP, block, heads * block), BF),
+        pltpu.VMEM((GROUP, cols, block), BF),
+        pltpu.VMEM((2, GROUP, 1, heads * block), F32),
+    ]
     state = pl.pallas_call(
         functools.partial(tiles_body, heads, tcap, n_rel, 0, False),
         in_specs=[SMEM, SMEM, SMEM] + [VMEM] * 6,
         out_specs=[VMEM] * 3,
         out_shape=state_shapes,
+        scratch_shapes=stage,
         name="near_tiles",
     )(order, ends, prior, bits, queries_t, keys, values_t, att_d, msg_d)
 
@@ -367,7 +393,7 @@
         in_specs=[SMEM, SMEM, SMEM] + [VMEM] * 9,
         out_specs=VMEM,
         out_shape=jax.ShapeDtypeStruct((blocks, cols + TAIL, block), BF),
-        scratch_shapes=[pltpu.VMEM(s.shape, s.dtype) for s in state_shapes],
+        scratch_shapes=[pltpu.VMEM(s.shape, s.dtype) for s in state_shapes] + stage,
         name="far_tiles",
     )(order, ends, prior, bits, queries_t, joined(far_keys), joined(far_values), att_d, msg_d, *state)
 
@@ -405,6 +431,4 @@
         P("rel", "node"),
     )
     out_specs = P(("node", "head"), None)
-    return jax.shard_map(
-        per_device, mesh=mesh, in_specs=in_specs, out_specs=out_specs, check_vma=False
-    )
+    return jax.shard_map(layer, mesh=mesh, in_specs=in_specs, out_specs=out_specs, check_vma=False)

time: 136 us -> 102 us (0.75)
  Pallas kernels: 73.2 us -> 37.4 us
  starting transfers between devices: 10 us -> 12.5 us
    pallas_call x5, Pallas kernels: 73.2 us -> 37.4 us  [the longest x1 11 us: layer(): pl.pallas_call(functools.partial(tiles_body, heads, tcap, n_rel, 1, True)...]
    all_to_all x1, starting transfers between devices: 3.58 us -> 6.07 us  [layer(): got = lax.all_to_all(send, ('rel', 'head'), 0, 0, tiled=True)]
  transfers between devices with their start and end apart: 6 -> 6, of which waited for: 3 -> 3; matrix products, arithmetic and copies ran while one was open for 6% -> 8% of each run, Pallas kernels for 28% -> 17%
where the time goes in v2:
time: 102 us
  Pallas kernels  37.4 us (37%)
  waiting for transfers between devices  23.5 us (23%)
  blocking collectives  16.7 us (16%)
  starting transfers between devices  12.5 us (12%)
  local copies, waits for them, and re-layouts  7.15 us (7%)
  other arithmetic  4.19 us (4%)
    ppermute x3, waiting for transfers between devices, layer(): lax.ppermute(w_out, 'head', shifted(n_head, s))  23.5 us
    all_gather x1, blocking collectives, layer(): return lax.all_gather(finished, 'rel', axis=0, tiled=True)  16.7 us
    pallas_call x1, Pallas kernels, layer(): pl.pallas_call(functools.partial(tiles_body, heads, tcap, n_rel, 1, True)...  11 us
    pallas_call x1, Pallas kernels, layer(): pl.pallas_call(functools.partial(tiles_body, heads, tcap, n_rel, 0, False...  10.1 us
    pallas_call x1, Pallas kernels, layer(): pl.pallas_call(q_body, grid_spec=pltpu.PrefetchScalarGridSpec(num_scalar_...  7.44 us
    all_to_all x1, starting transfers between devices, layer(): got = lax.all_to_all(send, ('rel', 'head'), 0, 0, tiled=True)  6.07 us
    pallas_call x1, Pallas kernels, layer(): pl.pallas_call(kv_body, grid=(blocks // step,), in_specs=[x_spec, kinds_s...  5.75 us
    ppermute x3, starting transfers between devices, layer(): lax.ppermute(w_out, 'head', shifted(n_head, s))  3.44 us
  transfers between devices with their start and end apart: 6, of which 3 were waited for; matrix products, arithmetic and copies ran while one was open for 8% of the time, Pallas kernels for 17%

profile of v2, /device:TPU:0, one launch (start us, length us, event | category | flops | bytes accessed | tf_op | source)
XLA Modules:
  0.0 101.6 jit_solution(2864724204318523732)
XLA Ops:
  0.0 5.8 %keys_values.1 = (bf16[16,128,128]{2,1,0:T(8,128)(2,1)}, bf16[16,128,128]{2,1,0:T(8,128)(2,1)}) custom-call(bf16[2048,512]{1,0:T(8,128)(2,1)} %x_ref.3, s32[4,4,128]{2,1,0:T(4,128)} %bitcast.11, bf16[4,512,128]{2,1,0:T(8,128)(2,1)} %wk_ref.1, bf16[4,512,128]{2,1,0:T(8,128)(2,1)} %wv_ref.1), custom_call_target="tpu_custom_call" | custom-call | tf_op jit(solution)/shard_map/keys_values/pallas_call | solution.py:322
  5.8 3.0 %collective-permute-start = (bf16[16,128,128]{2,1,0:T(8,128)(2,1)}, bf16[16,128,128]{2,1,0:T(8,128)(2,1)S(1)}, u32[]{:S(2)}, u32[]{:S(2)}) collective-permute-start(bf16[16,128,128]{2,1,0:T(8,128)(2,1)} %get-tuple-element.14.k_ref), channel_id=1, source_target_pairs={{0,4},{4,0},{1,5},{5,1},{2,6},{6,2},{3,7},{7,3},{8,12},{12,8},{9,1... | collective-permute-start | bytes 1572872 | tf_op jit(solution)/shard_map/ppermute | solution.py:334
  8.9 0.1 lt.77
  9.0 0.1 reshape.158
  9.1 0.7 convert_reduce_fusion.2
  9.8 0.1 convert_reduce_fusion.1
  10.0 0.1 copy.18
  10.2 0.6 gather_fusion
  10.7 0.6 mul.27.prior_ref
  11.4 7.4 %queries.1 = (bf16[16,128,128]{2,1,0:T(8,128)(2,1)}, bf16[16,128,128]{2,1,0:T(8,128)(2,1)}, bf16[16,128,128]{2,1,0:T(8,128)(2,1)}) custom-call(s32[16]{0:T(128)} %perm_ref.1, bf16[2048,512]{1,0:T(8,128)(2,1)} %x_ref.3, s32[4,4,128]{2,1,0:T(4,128)} %bitcast.12, bf16[4,512,128]{2,1,0:T(8,128)(2,1)} %wq_ref.1, bf16[64,2,64,64]{3,2,1,0:T(8,128)(2,1)} %att_ref.1, ...), custom_call_target="tpu_custom_call" | custom-call | tf_op jit(solution)/shard_map/queries/pallas_call | solution.py:338
  18.8 1.8 %pad_add_fusion.ends_ref = s32[2]{0:T(128)} fusion(s32[1]{0:T(128)} %bitcast.3, s32[1]{0:T(128)} %bitcast.2), kind=kLoop, calls=%fused_computation.43 | loop fusion | flops 2 | bytes 16 | tf_op jit(solution)/shard_map/stack | solution.py:281
  20.6 0.1 convert_reduce_fusion
  20.7 0.6 or_or_fusion
  21.4 0.7 select_reduce_fusion.list_ref
  22.0 10.1 %near_tiles.1 = (f32[16,1,256]{2,1,0:T(1,128)}, f32[16,1,256]{2,1,0:T(1,128)}, f32[16,128,128]{2,1,0:T(8,128)}) custom-call(s32[256]{0:T(256)} %select_reduce_fusion.list_ref, s32[2]{0:T(128)} %pad_add_fusion.ends_ref, f32[32]{0:T(128)} %mul.27.prior_ref, s32[256,4,128]{2,1,0:T(4,128)} %bitcast.9, bf16[16,128,128]{2,1,0:T(8,128)(2,1)} %get-tuple-element.13.qt_ref, ...), custom_call_target="tpu_custom_call" | custom-call | tf_op jit(solution)/shard_map/near_tiles/pallas_call | solution.py:379
  32.1 0.8 copy-done.1
  32.9 0.2 copy-done.2
  33.1 11.0 %far_tiles.1 = bf16[16,144,128]{2,1,0:T(8,128)(2,1)} custom-call(s32[256]{0:T(256)} %select_reduce_fusion.list_ref, s32[2]{0:T(128)} %pad_add_fusion.ends_ref, f32[32]{0:T(128)} %mul.27.prior_ref, s32[256,4,128]{2,1,0:T(4,128)} %bitcast.10, bf16[16,128,128]{2,1,0:T(8,128)(2,1)} %get-tuple-element.13.qt_ref, bf16[16,128,128]{2,1,0:T(8,128)(2,1)} %copy-done.1, ...), custom_call_target="tpu_custom_call" | custom-call | tf_op jit(solution)/shard_map/far_tiles/pallas_call | solution.py:391
  44.1 6.1 %all-to-all-start = ((bf16[16,144,128]{2,1,0:T(8,128)(2,1)}), bf16[16,144,128]{2,1,0:T(8,128)(2,1)S(1)}, u32[]{:S(2)}, u32[]{:S(2)}) async-start(bf16[16,144,128]{2,1,0:T(8,128)(2,1)} %far_tiles.1), calls=%async_computation | async-start | bytes 1179648 | tf_op jit(solution)/shard_map/all_to_all | solution.py:400
  50.2 0.5 collective-permute-start.2
  50.6 1.6 %collective-permute-start.3 = (bf16[4,128,512]{2,1,0:T(8,128)(2,1)S(1)}, bf16[4,128,512]{2,1,0:T(8,128)(2,1)S(1)}, u32[]{:S(2)}, u32[]{:S(2)}) collective-permute-start(bf16[4,128,512]{2,1,0:T(8,128)(2,1)S(1)} %copy-done.3), channel_id=1, source_target_pairs={{0,2},{1,3},{2,0},{3,1},{4,6},{5,7},{6,4},{7,5},{8,10},{9,11},{10,... | collective-permute-start | bytes 1572872 | tf_op jit(solution)/shard_map/ppermute | solution.py:313
  52.3 1.4 %collective-permute-start.4 = (bf16[4,128,512]{2,1,0:T(8,128)(2,1)S(1)}, bf16[4,128,512]{2,1,0:T(8,128)(2,1)S(1)}, u32[]{:S(2)}, u32[]{:S(2)}) collective-permute-start(bf16[4,128,512]{2,1,0:T(8,128)(2,1)S(1)} %copy-done.3), channel_id=1, source_target_pairs={{0,3},{1,0},{2,1},{3,2},{4,7},{5,4},{6,5},{7,6},{8,11},{9,8},{10,9... | collective-permute-start | bytes 1572872 | tf_op jit(solution)/shard_map/ppermute | solution.py:313
  53.6 1.3 %constant_dynamic-slice_fusion.1.kinds_ref = s32[1,128]{1,0:T(1,128)} fusion(s32[16,128]{1,0:T(8,128)} %bitcast.13, s32[]{:T(128)S(6)} %select_n.90), kind=kLoop, calls=%fused_computation.47 | loop fusion | bytes 1028 | tf_op jit(solution)/shard_map/dynamic_slice | solution.py:404
  54.9 1.6 %constant_dynamic-slice_fusion.x_ref = bf16[128,512]{1,0:T(8,128)(2,1)} fusion(bf16[2048,512]{1,0:T(8,128)(2,1)} %x_ref.3, s32[]{:T(128)S(6)} %select_n.89), kind=kLoop, calls=%fused_computation.46 | loop fusion | bytes 262148 | tf_op jit(solution)/shard_map/dynamic_slice | solution.py:403
  56.5 13.8 %collective-permute-done.2.refs_1_ = bf16[4,128,512]{2,1,0:T(8,128)(2,1)S(1)} collective-permute-done((bf16[4,128,512]{2,1,0:T(8,128)(2,1)S(1)}, bf16[4,128,512]{2,1,0:T(8,128)(2,1)S(1)}, u32[]{:S(2)}, u32[]{:S(2)}) %collective-permute-start.2) | collective-permute-done | bytes 524320 | tf_op jit(solution)/shard_map/ppermute | solution.py:313
  70.2 1.1 %collective-permute-done.3.refs_2_ = bf16[4,128,512]{2,1,0:T(8,128)(2,1)S(1)} collective-permute-done((bf16[4,128,512]{2,1,0:T(8,128)(2,1)S(1)}, bf16[4,128,512]{2,1,0:T(8,128)(2,1)S(1)}, u32[]{:S(2)}, u32[]{:S(2)}) %collective-permute-start.3) | collective-permute-done | bytes 524320 | tf_op jit(solution)/shard_map/ppermute | solution.py:313
  71.4 8.6 %collective-permute-done.4.refs_3_ = bf16[4,128,512]{2,1,0:T(8,128)(2,1)S(1)} collective-permute-done((bf16[4,128,512]{2,1,0:T(8,128)(2,1)S(1)}, bf16[4,128,512]{2,1,0:T(8,128)(2,1)S(1)}, u32[]{:S(2)}, u32[]{:S(2)}) %collective-permute-start.4) | collective-permute-done | bytes 524320 | tf_op jit(solution)/shard_map/ppermute | solution.py:313
  80.0 0.8 copy-done.6
  80.8 0.2 copy-done
  81.0 3.1 %finish.1 = bf16[128,512]{1,0:T(8,128)(2,1)} custom-call(s32[1]{0:T(128)} %bitcast.me_ref, f32[4]{0:T(128)} %skip_ref.1, bf16[16,144,128]{2,1,0:T(8,128)(2,1)} %copy-done, bf16[128,512]{1,0:T(8,128)(2,1)} %constant_dynamic-slice_fusion.x_ref, s32[1,128]{1,0:T(1,128)} %constant_dynamic-slice_fusion.1.kinds_ref, bf16[4,128,512]{2,1,0:T(8,128)(2,1)} %refs_0_.1, ...), custom_call_target="tpu_custom_call" | custom-call | tf_op jit(solution)/shard_map/finish/pallas_call | solution.py:405
  84.1 16.7 %all_gather.3 = bf16[512,512]{1,0:T(8,128)(2,1)S(1)} all-gather(bf16[128,512]{1,0:T(8,128)(2,1)} %finish.1), channel_id=1, replica_groups=mesh['rel'=4,'node'=2,'head'=4] {'rel'}, dimensions={0}, use_global_device_ids=true | all-gather | bytes 655360 | tf_op jit(solution)/shard_map/all_gather | solution.py:412
  100.8 0.8 copy.20
  (32 shorter events, 0.3 us)
Async XLA Ops:
  0.0 8.8 %copy-start.9 = (s32[16,1]{0,1:T(1,128)S(1)}, s32[16,1]{0,1:T(1,128)}, u32[]{:S(2)}) copy-start(s32[16,1]{0,1:T(1,128)} %param.29) | copy-start | bytes 196
  0.0 9.0 %copy-start.7 = (s32[16,16]{1,0:T(8,128)S(1)}, s32[16,16]{1,0:T(8,128)}, u32[]{:S(2)}) copy-start(s32[16,16]{1,0:T(8,128)} %param.26) | copy-start | bytes 3076
  0.0 9.9 %copy-start.8 = (s32[16,16]{1,0:T(8,128)S(1)}, s32[16,16]{1,0:T(8,128)}, u32[]{:S(2)}) copy-start(s32[16,16]{1,0:T(8,128)} %param.27) | copy-start | bytes 3076
  0.0 10.0 %copy-start.10 = (f32[64,2]{0,1:T(2,128)S(1)}, f32[64,2]{0,1:T(2,128)}, u32[]{:S(2)}) copy-start(f32[64,2]{0,1:T(2,128)} %param.22) | copy-start | bytes 1540
  0.0 10.1 %copy-start.11 = (s32[16]{0:T(128)S(1)}, s32[16]{0:T(128)}, u32[]{:S(2)}) copy-start(s32[16]{0:T(128)} %perm_ref.1) | copy-start | bytes 196
  5.8 26.3 %collective-permute-start = (bf16[16,128,128]{2,1,0:T(8,128)(2,1)}, bf16[16,128,128]{2,1,0:T(8,128)(2,1)S(1)}, u32[]{:S(2)}, u32[]{:S(2)}) collective-permute-start(bf16[16,128,128]{2,1,0:T(8,128)(2,1)} %get-tuple-element.14.k_ref), channel_id=1, source_target_pairs={{0,4},{4,0},{1,5},{5,1},{2,6},{6,2},{3,7},{7,3},{8,12},{12,8},{9,1... | collective-permute-start | bytes 1572872 | tf_op jit(solution)/shard_map/ppermute | solution.py:334
  8.7 23.4 %collective-permute-start.1 = (bf16[16,128,128]{2,1,0:T(8,128)(2,1)}, bf16[16,128,128]{2,1,0:T(8,128)(2,1)S(1)}, u32[]{:S(2)}, u32[]{:S(2)}) collective-permute-start(bf16[16,128,128]{2,1,0:T(8,128)(2,1)} %get-tuple-element.15.vt_ref), channel_id=1, source_target_pairs={{0,4},{4,0},{1,5},{5,1},{2,6},{6,2},{3,7},{7,3},{8,12},{12,8},{9,1... | collective-permute-start | bytes 1572872 | tf_op jit(solution)/shard_map/ppermute | solution.py:335
  32.1 0.8 copy-start.1
  32.1 1.0 copy-start.2
  33.1 17.1 %copy-start.3 = (bf16[4,128,512]{2,1,0:T(8,128)(2,1)S(1)}, bf16[4,128,512]{2,1,0:T(8,128)(2,1)}, u32[]{:S(2)}) copy-start(bf16[4,128,512]{2,1,0:T(8,128)(2,1)} %refs_0_.1) | copy-start | bytes 1572868
  44.1 35.9 %all-to-all-start = ((bf16[16,144,128]{2,1,0:T(8,128)(2,1)}), bf16[16,144,128]{2,1,0:T(8,128)(2,1)S(1)}, u32[]{:S(2)}, u32[]{:S(2)}) async-start(bf16[16,144,128]{2,1,0:T(8,128)(2,1)} %far_tiles.1), calls=%async_computation | async-start | bytes 1179648 | tf_op jit(solution)/shard_map/all_to_all | solution.py:400
  50.2 20.1 %collective-permute-start.2 = (bf16[4,128,512]{2,1,0:T(8,128)(2,1)S(1)}, bf16[4,128,512]{2,1,0:T(8,128)(2,1)S(1)}, u32[]{:S(2)}, u32[]{:S(2)}) collective-permute-start(bf16[4,128,512]{2,1,0:T(8,128)(2,1)S(1)} %copy-done.3), channel_id=1, source_target_pairs={{0,1},{1,2},{2,3},{3,0},{4,5},{5,6},{6,7},{7,4},{8,9},{9,10},{10,1... | collective-permute-start | bytes 1572872 | tf_op jit(solution)/shard_map/ppermute | solution.py:313
  50.6 20.8 %collective-permute-start.3 = (bf16[4,128,512]{2,1,0:T(8,128)(2,1)S(1)}, bf16[4,128,512]{2,1,0:T(8,128)(2,1)S(1)}, u32[]{:S(2)}, u32[]{:S(2)}) collective-permute-start(bf16[4,128,512]{2,1,0:T(8,128)(2,1)S(1)} %copy-done.3), channel_id=1, source_target_pairs={{0,2},{1,3},{2,0},{3,1},{4,6},{5,7},{6,4},{7,5},{8,10},{9,11},{10,... | collective-permute-start | bytes 1572872 | tf_op jit(solution)/shard_map/ppermute | solution.py:313
  52.3 27.7 %collective-permute-start.4 = (bf16[4,128,512]{2,1,0:T(8,128)(2,1)S(1)}, bf16[4,128,512]{2,1,0:T(8,128)(2,1)S(1)}, u32[]{:S(2)}, u32[]{:S(2)}) collective-permute-start(bf16[4,128,512]{2,1,0:T(8,128)(2,1)S(1)} %copy-done.3), channel_id=1, source_target_pairs={{0,3},{1,0},{2,1},{3,2},{4,7},{5,4},{6,5},{7,6},{8,11},{9,8},{10,9... | collective-permute-start | bytes 1572872 | tf_op jit(solution)/shard_map/ppermute | solution.py:313
  70.2 9.7 %copy-start.4 = (bf16[4,128,512]{2,1,0:T(8,128)(2,1)}, bf16[4,128,512]{2,1,0:T(8,128)(2,1)S(1)}, u32[]{:S(2)}) copy-start(bf16[4,128,512]{2,1,0:T(8,128)(2,1)S(1)} %collective-permute-done.2.refs_1_) | copy-start | bytes 1572868
  71.4 8.6 %copy-start.5 = (bf16[4,128,512]{2,1,0:T(8,128)(2,1)}, bf16[4,128,512]{2,1,0:T(8,128)(2,1)S(1)}, u32[]{:S(2)}) copy-start(bf16[4,128,512]{2,1,0:T(8,128)(2,1)S(1)} %collective-permute-done.3.refs_2_) | copy-start | bytes 1572868
  80.0 0.8 copy-start.6
  80.0 1.0 copy-start

commit v3 on v2

--- a/solution.py
+++ b/solution.py
@@ -20,6 +20,7 @@
 VMEM = pl.BlockSpec(memory_space=pltpu.VMEM)
 SMEM = pl.BlockSpec(memory_space=pltpu.SMEM)
 ANY = pl.BlockSpec(memory_space=pl.ANY)
+SMALL = pltpu.CompilerParams(vmem_limit_bytes=16 << 20)
 
 
 def hits_of(kinds_row, types):
@@ -57,16 +58,15 @@
         vt_ref[b] = part[:, cols:].T.astype(BF)
 
 
-def q_body(perm_ref, x_ref, kinds_ref, wq_ref, att_ref, msg_ref, qt_ref, attd_ref, msgd_ref, att_s, msg_s, sems):
+def q_body(perm_ref, x_ref, kinds_ref, wq_ref, att_ref, msg_ref, qt_ref, atts_ref, msgt_ref, msg_s, sems):
     types = wq_ref.shape[0]
-    positions = attd_ref.shape[0]
-    heads, hd = att_ref.shape[1], att_ref.shape[2]
+    positions, heads = msg_s.shape[:2]
     step = qt_ref.shape[0]
 
     def copies(p):
         r = perm_ref[p]
         return (
-            pltpu.make_async_copy(att_ref.at[r], att_s.at[p], sems.at[0, p]),
+            pltpu.make_async_copy(att_ref.at[r], atts_ref.at[p], sems.at[0, p]),
             pltpu.make_async_copy(msg_ref.at[r], msg_s.at[p], sems.at[1, p]),
         )
 
@@ -88,39 +88,71 @@
                 copy.wait()
         for p in range(positions):
             for h in range(heads):
-                pads = [jnp.zeros((hd, hd), F32)] * heads
-                lanes = list(pads)
-                lanes[h] = att_s[p, h].astype(F32)
-                attd_ref[p, h * hd : (h + 1) * hd, :] = jnp.concatenate(lanes, axis=1).astype(BF)
-                lanes = list(pads)
-                lanes[h] = msg_s[p, h].astype(F32).T
-                msgd_ref[p, h * hd : (h + 1) * hd, :] = jnp.concatenate(lanes, axis=1).astype(BF)
-
-
-def tiles_body(
-    heads, tcap, n_rel, first, last, list_ref, ends_ref, prior_ref, bits_ref, qt_ref, k_ref, vt_ref, attd_ref, msgd_ref, *refs
+                msgt_ref[p, h] = msg_s[p, h].astype(F32).T.astype(BF)
+
+
+def split(x, n):
+    if n & (n - 1) == 0:
+        return x >> (n.bit_length() - 1), x & (n - 1)
+    return lax.div(x, n), lax.rem(x, n)
+
+
+def build_lists(n_node, blocks, me, src_ref, dst_ref, count_ref, near_ref, far_ref, ends_ref):
+    positions, tcap = src_ref.shape
+
+    def one(p, found):
+        n_near, n_far = found
+        count = count_ref[p, 0]
+        for k in range(tcap):
+            owner, place = split(src_ref[p, k], blocks)
+            _, away = split(me + n_node - owner, n_node)
+            code = (p * tcap + k) | (dst_ref[p, k] << 24)
+            near_ref[n_near] = code | (place << 12)
+            far_ref[n_far] = code | ((place + (away - 1) * blocks) << 12)
+            live = k < count
+            n_near = n_near + jnp.where(jnp.logical_and(live, away == 0), 1, 0)
+            n_far = n_far + jnp.where(jnp.logical_and(live, away != 0), 1, 0)
+        return n_near, n_far
+
+    n_near, n_far = lax.fori_loop(0, positions, one, (jnp.int32(0), jnp.int32(0)))
+    ends_ref[0] = n_near
+    ends_ref[1] = n_far
+
+
+def near_body(n_node, me_ref, src_ref, dst_ref, count_ref, perm_ref, prior_ref, bits_ref, qt_ref, k_ref, vt_ref, atts_ref, msgt_ref, m_ref, l_ref, a_ref, far_ref, ends_ref, near_s, *stage):
+    build_lists(n_node, qt_ref.shape[0], me_ref[0], src_ref, dst_ref, count_ref, near_s, far_ref, ends_ref)
+    m_ref[...] = jnp.full(m_ref.shape, FLOOR, F32)
+    l_ref[...] = jnp.zeros(l_ref.shape, F32)
+    a_ref[...] = jnp.zeros(a_ref.shape, F32)
+    visit_tiles(near_s, ends_ref[0], src_ref.shape[1], perm_ref, prior_ref, bits_ref, qt_ref, k_ref, vt_ref, atts_ref, msgt_ref, m_ref, l_ref, a_ref, *stage)
+
+
+def far_body(n_rel, tcap, far_ref, ends_ref, perm_ref, prior_ref, bits_ref, qt_ref, k_ref, vt_ref, atts_ref, msgt_ref, m_in, l_in, a_in, send_ref, m_ref, l_ref, a_ref, *stage):
+    visit_tiles(far_ref, ends_ref[1], tcap, perm_ref, prior_ref, bits_ref, qt_ref, k_ref, vt_ref, atts_ref, msgt_ref, m_ref, l_ref, a_ref, *stage)
+    heads, cols = prior_ref.shape[0], qt_ref.shape[1]
+    blocks = a_ref.shape[0]
+    n_head = blocks // n_rel
+    for b in range(blocks):
+        spot = (b % n_rel) * n_head + b // n_rel
+        send_ref[spot, :cols, :] = a_ref[b].astype(BF)
+        rows = []
+        for value in (m_ref[b], l_ref[b]):
+            rest = value
+            for _ in range(3):
+                piece = rest.astype(BF).astype(F32)
+                rest = rest - piece
+                rows += [piece[:, h * LANES : (h + 1) * LANES] for h in range(heads)]
+        rows.append(jnp.zeros((TAIL - len(rows), LANES), F32))
+        send_ref[spot, cols:, :] = jnp.concatenate(rows, axis=0).astype(BF)
+
+
+def visit_tiles(
+    list_ref, count, tcap, perm_ref, prior_ref, bits_ref, qt_ref, k_ref, vt_ref, atts_ref, msgt_ref, m_ref, l_ref, a_ref, q_s, w_s, v_s, t_s
 ):
-    if first == 0:
-        start = 0
-    else:
-        start = ends_ref[first - 1]
-        old_m, old_l, old_a, *refs = refs
-    stop = ends_ref[first]
-    *refs, q_s, w_s, v_s, t_s = refs
-    if last:
-        send_ref, m_ref, l_ref, a_ref = refs
-    else:
-        m_ref, l_ref, a_ref = refs
+    heads = prior_ref.shape[0]
     cols = qt_ref.shape[1]
     hd = cols // heads
-    if first == 0:
-        m_ref[...] = jnp.full(m_ref.shape, FLOOR, F32)
-        l_ref[...] = jnp.zeros(l_ref.shape, F32)
-        a_ref[...] = jnp.zeros(a_ref.shape, F32)
-    else:
-        m_ref[...] = old_m[...]
-        l_ref[...] = old_l[...]
-        a_ref[...] = old_a[...]
+    factor = 1.0 / math.sqrt(hd)
     q_s[...] = jnp.zeros(q_s.shape, BF)
     w_s[...] = jnp.zeros(w_s.shape, BF)
     v_s[...] = jnp.zeros(v_s.shape, BF)
@@ -129,12 +161,17 @@
     shift = 31 - lax.broadcasted_iota(jnp.int32, (32, LANES), 0)
 
     def read(index):
-        code = list_ref[jnp.clip(index, start, stop - 1)]
+        code = list_ref[jnp.clip(index, 0, count - 1)]
         slot = code & 0xFFF
-        return slot, (code >> 12) & 0xFFF, code >> 24, lax.div(slot, tcap)
+        return slot, (code >> 12) & 0xFFF, code >> 24, split(slot, tcap)[0]
+
+    def by_head(left, right):
+        return [
+            jnp.dot(left[h], right[h * hd : (h + 1) * hd], preferred_element_type=F32) for h in range(heads)
+        ]
 
     def visit(turn, carry):
-        base = start + turn * GROUP
+        base = turn * GROUP
         sums, scores, messages, queries = [], [], [], []
         for g in range(GROUP):
             sums.append(
@@ -150,10 +187,10 @@
         for g in range(GROUP):
             slot, src, dst, position = read(base - GROUP + g)
             scores.append(jnp.dot(k_ref[src], q_s[g], preferred_element_type=F32))
-            messages.append(jnp.dot(msgd_ref[position], vt_ref[src], preferred_element_type=F32))
+            messages.append(by_head(msgt_ref[position], vt_ref[src]))
         for g in range(GROUP):
             slot, src, dst, position = read(base + g)
-            queries.append(jnp.dot(attd_ref[position], qt_ref[dst], preferred_element_type=F32))
+            queries.append(by_head(atts_ref[position], qt_ref[dst]))
         for g in range(GROUP):
             slot, src, dst, position = read(base - 2 * GROUP + g)
             top, total = t_s[0, g], t_s[1, g]
@@ -170,7 +207,7 @@
         for g in range(GROUP):
             index = base - GROUP + g
             slot, src, dst, position = read(index)
-            valid = jnp.logical_and(index >= start, index < stop)
+            valid = jnp.logical_and(index >= 0, index < count)
             words = jnp.where(valid, bits_ref[slot], 0)
             parts = []
             for w in range(words.shape[0]):
@@ -183,33 +220,17 @@
             t_s[0, g] = top
             t_s[1, g] = jnp.sum(weights, axis=0, keepdims=True)
             w_s[g] = weights.astype(BF)
-            v_s[g] = messages[g].astype(BF)
+            for h in range(heads):
+                v_s[g, h * hd : (h + 1) * hd, :] = messages[g][h].astype(BF)
         for g in range(GROUP):
             slot, src, dst, position = read(base + g)
             for h in range(heads):
                 rows = slice(h * hd, (h + 1) * hd)
-                piece = queries[g][rows] * prior_ref[position * heads + h]
-                q_s[g, rows, h * LANES : (h + 1) * LANES] = piece.astype(BF)
+                scale = prior_ref[h, perm_ref[position]] * factor
+                q_s[g, rows, h * LANES : (h + 1) * LANES] = (queries[g][h] * scale).astype(BF)
         return carry
 
-    count = stop - start
     lax.fori_loop(0, jnp.where(count > 0, lax.div(count + GROUP - 1, GROUP) + 2, 0), visit, 0)
-
-    if last:
-        blocks = a_ref.shape[0]
-        n_head = blocks // n_rel
-        for b in range(blocks):
-            spot = (b % n_rel) * n_head + b // n_rel
-            send_ref[spot, :cols, :] = a_ref[b].astype(BF)
-            rows = []
-            for value, count in ((m_ref[b], 3), (l_ref[b], 3)):
-                rest = value
-                for _ in range(count):
-                    piece = rest.astype(BF).astype(F32)
-                    rest = rest - piece
-                    rows += [piece[:, h * LANES : (h + 1) * LANES] for h in range(heads)]
-            rows.append(jnp.zeros((TAIL - len(rows), LANES), F32))
-            send_ref[spot, cols:, :] = jnp.concatenate(rows, axis=0).astype(BF)
 
 
 def finish_body(heads, n_rel, n_head, me_ref, skip_ref, got_ref, x_ref, kinds_ref, *refs):
@@ -255,30 +276,16 @@
     out_ref[...] = (gate * mixed + (1.0 - gate) * x_ref[...].astype(F32)).astype(BF)
 
 
+def onchip(x):
+    return pltpu.with_memory_space_constraint(x, pltpu.VMEM)
+
+
+def offchip(x):
+    return pltpu.with_memory_space_constraint(x, pltpu.HBM)
+
+
 def shifted(n, s):
     return [(i, (i + s) % n) for i in range(n)]
-
-
-def listed(tile_src, tile_dst, tile_count, blocks, me, n_node):
-    positions, tcap = tile_src.shape
-    slots = positions * tcap
-    src = tile_src.reshape(slots)
-    dst = tile_dst.reshape(slots)
-    ids = jnp.arange(slots, dtype=jnp.int32)
-    live = (jnp.arange(tcap, dtype=jnp.int32)[None, :] < tile_count).reshape(slots)
-    away = (me - src // blocks) % n_node
-    near = live & (away == 0)
-    far = live & (away != 0)
-    place = src % blocks + jnp.maximum(away - 1, 0) * blocks
-    code = ids | (place << 12) | (dst << 24)
-    n_near = jnp.sum(near.astype(jnp.int32))
-    n_live = jnp.sum(live.astype(jnp.int32))
-    before = ids[None, :] < ids[:, None]
-    near_rank = jnp.sum((before & near[None, :]).astype(jnp.int32), axis=1)
-    far_rank = jnp.sum((before & far[None, :]).astype(jnp.int32), axis=1)
-    rank = jnp.where(near, near_rank, jnp.where(far, n_near + far_rank, -1))
-    order = jnp.sum(jnp.where(rank[None, :] == ids[:, None], code[None, :], 0), axis=1)
-    return order, jnp.stack([n_near, n_live])
 
 
 def layer(
@@ -318,24 +325,25 @@
     w_spec = pl.BlockSpec((types, depth, cols), lambda i: (0, 0, 0))
     b_spec = pl.BlockSpec((step, block, cols), lambda i: (i, 0, 0))
     bt_spec = pl.BlockSpec((step, cols, block), lambda i: (i, 0, 0))
-    kinds_in = kinds.reshape(blocks // step, step, block)
+    kinds_in = offchip(kinds.reshape(blocks // step, step, block))
     keys, values_t = pl.pallas_call(
         kv_body,
         grid=(blocks // step,),
         in_specs=[x_spec, kinds_spec, w_spec, w_spec],
         out_specs=[b_spec, bt_spec],
         out_shape=[
-            jax.ShapeDtypeStruct((blocks, block, cols), BF),
-            jax.ShapeDtypeStruct((blocks, cols, block), BF),
+            pltpu.VMEM((blocks, block, cols), BF),
+            pltpu.VMEM((blocks, cols, block), BF),
         ],
+        compiler_params=SMALL,
         name="keys_values",
-    )(features, kinds_in, w_key, w_value)
+    )(offchip(features), kinds_in, offchip(w_key), offchip(w_value))
 
     far_keys = [lax.ppermute(keys, "node", shifted(n_node, s)) for s in range(1, n_node)]
     far_values = [lax.ppermute(values_t, "node", shifted(n_node, s)) for s in range(1, n_node)]
 
-    d_spec = pl.BlockSpec((positions, cols, cols), lambda i, perm: (0, 0, 0))
-    queries_t, att_d, msg_d = pl.pallas_call(
+    d_spec = pl.BlockSpec((positions, heads, hd, hd), lambda i, perm: (0, 0, 0, 0))
+    queries_t, atts, msgs_t = pl.pallas_call(
         q_body,
         grid_spec=pltpu.PrefetchScalarGridSpec(
             num_scalar_prefetch=1,
@@ -350,25 +358,25 @@
             out_specs=[pl.BlockSpec((step, cols, block), lambda i, perm: (i, 0, 0)), d_spec, d_spec],
             scratch_shapes=[
                 pltpu.VMEM((positions, heads, hd, hd), BF),
-                pltpu.VMEM((positions, heads, hd, hd), BF),
                 pltpu.SemaphoreType.DMA((2, positions)),
             ],
         ),
         out_shape=[
-            jax.ShapeDtypeStruct((blocks, cols, block), BF),
-            jax.ShapeDtypeStruct((positions, cols, cols), BF),
-            jax.ShapeDtypeStruct((positions, cols, cols), BF),
+            pltpu.VMEM((blocks, cols, block), BF),
+            pltpu.VMEM((positions, heads, hd, hd), BF),
+            pltpu.VMEM((positions, heads, hd, hd), BF),
         ],
+        compiler_params=SMALL,
         name="queries",
-    )(rel_perm, features, kinds_in, w_query, rel_att, rel_msg)
-
-    order, ends = listed(tile_src, tile_dst, tile_count, blocks, lax.axis_index("node"), n_node)
-    prior = (rel_prior[rel_perm] * (1.0 / math.sqrt(hd))).reshape(positions * heads)
+    )(rel_perm, offchip(features), kinds_in, offchip(w_query), offchip(rel_att), offchip(rel_msg))
+
+    me = lax.axis_index("node").reshape(1)
+    prior = rel_prior.T
     bits = tile_bits.transpose(0, 1, 3, 2).reshape(slots, words, block)
     state_shapes = [
-        jax.ShapeDtypeStruct((blocks, 1, heads * block), F32),
-        jax.ShapeDtypeStruct((blocks, 1, heads * block), F32),
-        jax.ShapeDtypeStruct((blocks, cols, block), F32),
+        pltpu.VMEM((blocks, 1, heads * block), F32),
+        pltpu.VMEM((blocks, 1, heads * block), F32),
+        pltpu.VMEM((blocks, cols, block), F32),
     ]
     stage = [
         pltpu.VMEM((GROUP, cols, heads * block), BF),
@@ -376,26 +384,31 @@
         pltpu.VMEM((GROUP, cols, block), BF),
         pltpu.VMEM((2, GROUP, 1, heads * block), F32),
     ]
-    state = pl.pallas_call(
-        functools.partial(tiles_body, heads, tcap, n_rel, 0, False),
-        in_specs=[SMEM, SMEM, SMEM] + [VMEM] * 6,
-        out_specs=[VMEM] * 3,
-        out_shape=state_shapes,
+    shared = [onchip(x) for x in (bits, queries_t, atts, msgs_t)]
+    *state, far_list, ends = pl.pallas_call(
+        functools.partial(near_body, n_node),
+        in_specs=[SMEM] * 6 + [VMEM] * 6,
+        out_specs=[VMEM] * 3 + [SMEM] * 2,
+        out_shape=state_shapes
+        + [jax.ShapeDtypeStruct((slots,), jnp.int32), jax.ShapeDtypeStruct((2,), jnp.int32)],
+        scratch_shapes=[pltpu.SMEM((slots,), jnp.int32)] + stage,
+        compiler_params=SMALL,
+        name="near_tiles",
+    )(me, tile_src, tile_dst, tile_count, rel_perm, prior, *shared[:2], onchip(keys), onchip(values_t), *shared[2:])
+
+    def joined(arrays):
+        return onchip(arrays[0] if len(arrays) == 1 else jnp.concatenate(arrays, axis=0))
+
+    send, *_ = pl.pallas_call(
+        functools.partial(far_body, n_rel, tcap),
+        in_specs=[SMEM] * 4 + [VMEM] * 9,
+        out_specs=[VMEM] * 4,
+        out_shape=[jax.ShapeDtypeStruct((blocks, cols + TAIL, block), BF)] + state_shapes,
+        input_output_aliases={10: 1, 11: 2, 12: 3},
         scratch_shapes=stage,
-        name="near_tiles",
-    )(order, ends, prior, bits, queries_t, keys, values_t, att_d, msg_d)
-
-    def joined(arrays):
-        return arrays[0] if len(arrays) == 1 else jnp.concatenate(arrays, axis=0)
-
-    send = pl.pallas_call(
-        functools.partial(tiles_body, heads, tcap, n_rel, 1, True),
-        in_specs=[SMEM, SMEM, SMEM] + [VMEM] * 9,
-        out_specs=VMEM,
-        out_shape=jax.ShapeDtypeStruct((blocks, cols + TAIL, block), BF),
-        scratch_shapes=[pltpu.VMEM(s.shape, s.dtype) for s in state_shapes] + stage,
+        compiler_params=SMALL,
         name="far_tiles",
-    )(order, ends, prior, bits, queries_t, joined(far_keys), joined(far_values), att_d, msg_d, *state)
+    )(far_list, ends, rel_perm, prior, *shared[:2], joined(far_keys), joined(far_values), *shared[2:], *state)
 
     got = lax.all_to_all(send, ("rel", "head"), 0, 0, tiled=True)
 
@@ -407,8 +420,9 @@
         in_specs=[SMEM, SMEM] + [VMEM] * (3 + n_head),
         out_specs=VMEM,
         out_shape=jax.ShapeDtypeStruct((block, depth), BF),
+        compiler_params=SMALL,
         name="finish",
-    )(lax.axis_index("head").reshape(1), skip, got, own_rows, own_kinds, *w_parts)
+    )(lax.axis_index("head").reshape(1), skip, *[onchip(x) for x in (got, own_rows, own_kinds, *w_parts)])
     return lax.all_gather(finished, "rel", axis=0, tiled=True)
 
 

time: 102 us -> 94.3 us (0.925)
  waiting for transfers between devices: 23.5 us -> 30.4 us
  Pallas kernels: 37.4 us -> 32.7 us
  local copies, waits for them, and re-layouts: 7.15 us -> 2.51 us
  other arithmetic: 4.19 us -> 0 us
    ppermute x1, waiting for transfers between devices: 0.01 us -> 5.69 us  [layer(): lax.ppermute(values_t, 'node', shifted(n_node, s))]
    unnamed x26 -> x18, local copies, waits for them, and re-layouts: 2.87 us -> 0.91 us
    pallas_call x1, Pallas kernels: 3.12 us -> 1.23 us  [layer(): pl.pallas_call(functools.partial(finish_body, heads, n_rel, n_head), in_s...]
    another operation x1 -> x0, other arithmetic: 1.79 us -> none  [listed(): return (order, jnp.stack([n_near, n_live]))]
    reduce_sum x4 -> x0, other arithmetic: 1.63 us -> none  [the longest x1 0.74 us: listed(): n_live = jnp.sum(live.astype(jnp.int32))]
    pallas_call x1, Pallas kernels: 7.44 us -> 6 us  [layer(): pl.pallas_call(q_body, grid_spec=pltpu.PrefetchScalarGridSpec(num_scalar_...]
    ppermute x3, waiting for transfers between devices: 23.5 us -> 24.7 us  [layer(): lax.ppermute(w_out, 'head', shifted(n_head, s))]
    all_to_all x1, starting transfers between devices: 6.07 us -> 5.03 us  [layer(): got = lax.all_to_all(send, ('rel', 'head'), 0, 0, tiled=True)]
  transfers between devices with their start and end apart: 6 -> 6, of which waited for: 3 -> 4; matrix products, arithmetic and copies ran while one was open for 8% -> 2% of each run, Pallas kernels for 17% -> 18%
where the time goes in v3:
time: 94.3 us; the launch traced here: 93.9 us
  Pallas kernels  32.7 us (35%)
  waiting for transfers between devices  30.4 us (32%)
  blocking collectives  16.5 us (17%)
  starting transfers between devices  11.6 us (12%)
  local copies, waits for them, and re-layouts  2.51 us (3%)
    ppermute x3, waiting for transfers between devices, layer(): lax.ppermute(w_out, 'head', shifted(n_head, s))  24.7 us
    all_gather x1, blocking collectives, layer(): return lax.all_gather(finished, 'rel', axis=0, tiled=True)  16.5 us
    pallas_call x1, Pallas kernels, layer(): pl.pallas_call(functools.partial(near_body, n_node), in_specs=[SMEM] * 6...  11.2 us
    pallas_call x1, Pallas kernels, layer(): pl.pallas_call(functools.partial(far_body, n_rel, tcap), in_specs=[SMEM]...  9.29 us
    pallas_call x1, Pallas kernels, layer(): pl.pallas_call(q_body, grid_spec=pltpu.PrefetchScalarGridSpec(num_scalar_...  6 us
    ppermute x1, waiting for transfers between devices, layer(): lax.ppermute(values_t, 'node', shifted(n_node, s))  5.69 us
    all_to_all x1, starting transfers between devices, layer(): got = lax.all_to_all(send, ('rel', 'head'), 0, 0, tiled=True)  5.03 us
    pallas_call x1, Pallas kernels, layer(): pl.pallas_call(kv_body, grid=(blocks // step,), in_specs=[x_spec, kinds_s...  5.01 us
  transfers between devices with their start and end apart: 6, of which 4 were waited for; matrix products, arithmetic and copies ran while one was open for 2% of the time, Pallas kernels for 18%

profile of v3, /device:TPU:0, one launch (start us, length us, event | category | flops | bytes accessed | tf_op | source)
XLA Modules:
  0.0 93.9 jit_solution(14837908847164861792)
XLA Ops:
  0.0 0.0 copy-start.7
  0.0 5.0 %keys_values.1 = (bf16[16,128,128]{2,1,0:T(8,128)(2,1)S(1)}, bf16[16,128,128]{2,1,0:T(8,128)(2,1)S(1)}) custom-call(bf16[2048,512]{1,0:T(8,128)(2,1)} %x_ref.3, s32[4,4,128]{2,1,0:T(4,128)} %bitcast.12, bf16[4,512,128]{2,1,0:T(8,128)(2,1)} %wk_ref.1, bf16[4,512,128]{2,1,0:T(8,128)(2,1)} %wv_ref.1), custom_call_target="tpu_custom_call" | custom-call | tf_op jit(solution)/shard_map/keys_values/pallas_call | solution.py:329
  5.0 3.0 %collective-permute-start = (bf16[16,128,128]{2,1,0:T(8,128)(2,1)S(1)}, bf16[16,128,128]{2,1,0:T(8,128)(2,1)S(1)}, u32[]{:S(2)}, u32[]{:S(2)}) collective-permute-start(bf16[16,128,128]{2,1,0:T(8,128)(2,1)S(1)} %get-tuple-element.17.k_ref), channel_id=1, source_target_pairs={{0,4},{4,0},{1,5},{5,1},{2,6},{6,2},{3,7},{7,3},{8,12},{12,8},{9,1... | collective-permute-start | bytes 1572872 | tf_op jit(solution)/shard_map/ppermute | solution.py:342
  8.1 0.1 collective-permute-start.1
  8.1 0.0 copy-done.7
  8.1 0.1 copy.19.count_ref
  8.2 0.0 copy-done.4
  8.2 0.0 copy-start.5
  8.2 6.0 %queries.1 = (bf16[16,128,128]{2,1,0:T(8,128)(2,1)S(1)}, bf16[16,2,64,64]{3,2,1,0:T(8,128)(2,1)S(1)}, bf16[16,2,64,64]{3,2,1,0:T(8,128)(2,1)S(1)}) custom-call(s32[16]{0:T(128)S(1)} %copy-done.4, bf16[2048,512]{1,0:T(8,128)(2,1)} %x_ref.3, s32[4,4,128]{2,1,0:T(4,128)} %bitcast.13, bf16[4,512,128]{2,1,0:T(8,128)(2,1)} %wq_ref.1, ...), custom_call_target="tpu_custom_call" | custom-call | tf_op jit(solution)/shard_map/queries/pallas_call | solution.py:346
  14.3 0.0 copy-done
  14.3 0.0 copy-done.2
  14.3 0.0 copy-done.3
  14.3 0.0 copy-done.5
  14.3 11.2 %near_tiles.1 = (f32[16,1,256]{2,1,0:T(1,128)S(1)}, f32[16,1,256]{2,1,0:T(1,128)S(1)}, f32[16,128,128]{2,1,0:T(8,128)S(1)}, s32[256]{0:T(256)S(1)}, s32[2]{0:T(128)S(1)}) custom-call(s32[1]{0:T(128)} %bitcast.1.me_ref, s32[16,16]{1,0:T(8,128)S(1)} %copy-done.2, s32[16,16]{1,0:T(8,128)S(1)} %copy-done.3, s32[16,1]{1,0:T(8,128)S(1)} %copy.19.count_ref, ...), custom_call_target="tpu_custom_call" | custom-call | tf_op jit(solution)/shard_map/near_tiles/pallas_call | solution.py:388
  25.5 0.0 collective-permute-done.k_ref
  25.5 5.7 %collective-permute-done.1.vt_ref = bf16[16,128,128]{2,1,0:T(8,128)(2,1)S(1)} collective-permute-done((bf16[16,128,128]{2,1,0:T(8,128)(2,1)S(1)}, bf16[16,128,128]{2,1,0:T(8,128)(2,1)S(1)}, u32[]{:S(2)}, u32[]{:S(2)}) %collective-permute-start.1) | collective-permute-done | bytes 524320 | tf_op jit(solution)/shard_map/ppermute | solution.py:343
  31.2 9.3 %far_tiles.1 = (bf16[16,144,128]{2,1,0:T(8,128)(2,1)}, f32[16,1,256]{2,1,0:T(1,128)S(1)}, f32[16,1,256]{2,1,0:T(1,128)S(1)}, f32[16,128,128]{2,1,0:T(8,128)S(1)}) custom-call(s32[256]{0:T(256)S(1)} %get-tuple-element.21.far_ref, s32[2]{0:T(128)S(1)} %get-tuple-element.22.ends_ref, ...), custom_call_target="tpu_custom_call", output_to_operand_aliasing={{1}: (10, {}), {2}: (11, {}), {3}: (12, {})} | custom-call | tf_op jit(solution)/shard_map/far_tiles/pallas_call | solution.py:402
  40.5 5.0 %all-to-all-start = ((bf16[16,144,128]{2,1,0:T(8,128)(2,1)}), bf16[16,144,128]{2,1,0:T(8,128)(2,1)S(1)}, u32[]{:S(2)}, u32[]{:S(2)}) async-start(bf16[16,144,128]{2,1,0:T(8,128)(2,1)} %get-tuple-element.26), calls=%async_computation | async-start | bytes 1179648 | tf_op jit(solution)/shard_map/all_to_all | solution.py:413
  45.5 0.0 copy-done.1
  45.6 0.5 collective-permute-start.2
  46.0 1.6 %collective-permute-start.3 = (bf16[4,128,512]{2,1,0:T(8,128)(2,1)S(1)}, bf16[4,128,512]{2,1,0:T(8,128)(2,1)S(1)}, u32[]{:S(2)}, u32[]{:S(2)}) collective-permute-start(bf16[4,128,512]{2,1,0:T(8,128)(2,1)S(1)} %copy-done.1), channel_id=1, source_target_pairs={{0,2},{1,3},{2,0},{3,1},{4,6},{5,7},{6,4},{7,5},{8,10},{9,11},{10,... | collective-permute-start | bytes 1572872 | tf_op jit(solution)/shard_map/ppermute | solution.py:320
  47.6 1.4 %collective-permute-start.4 = (bf16[4,128,512]{2,1,0:T(8,128)(2,1)S(1)}, bf16[4,128,512]{2,1,0:T(8,128)(2,1)S(1)}, u32[]{:S(2)}, u32[]{:S(2)}) collective-permute-start(bf16[4,128,512]{2,1,0:T(8,128)(2,1)S(1)} %copy-done.1), channel_id=1, source_target_pairs={{0,3},{1,0},{2,1},{3,2},{4,7},{5,4},{6,5},{7,6},{8,11},{9,8},{10,9... | collective-permute-start | bytes 1572872 | tf_op jit(solution)/shard_map/ppermute | solution.py:320
  49.0 0.7 constant_dynamic-slice_fusion.kinds_ref
  49.7 0.9 constant_dynamic-slice_fusion.1.x_ref
  50.6 15.0 %collective-permute-done.2.refs_1_ = bf16[4,128,512]{2,1,0:T(8,128)(2,1)S(1)} collective-permute-done((bf16[4,128,512]{2,1,0:T(8,128)(2,1)S(1)}, bf16[4,128,512]{2,1,0:T(8,128)(2,1)S(1)}, u32[]{:S(2)}, u32[]{:S(2)}) %collective-permute-start.2) | collective-permute-done | bytes 524320 | tf_op jit(solution)/shard_map/ppermute | solution.py:320
  65.6 1.1 %collective-permute-done.3.refs_2_ = bf16[4,128,512]{2,1,0:T(8,128)(2,1)S(1)} collective-permute-done((bf16[4,128,512]{2,1,0:T(8,128)(2,1)S(1)}, bf16[4,128,512]{2,1,0:T(8,128)(2,1)S(1)}, u32[]{:S(2)}, u32[]{:S(2)}) %collective-permute-start.3) | collective-permute-done | bytes 524320 | tf_op jit(solution)/shard_map/ppermute | solution.py:320
  66.8 8.6 %collective-permute-done.4.refs_3_ = bf16[4,128,512]{2,1,0:T(8,128)(2,1)S(1)} collective-permute-done((bf16[4,128,512]{2,1,0:T(8,128)(2,1)S(1)}, bf16[4,128,512]{2,1,0:T(8,128)(2,1)S(1)}, u32[]{:S(2)}, u32[]{:S(2)}) %collective-permute-start.4) | collective-permute-done | bytes 524320 | tf_op jit(solution)/shard_map/ppermute | solution.py:320
  75.3 0.0 all-to-all-done.got_ref
  75.3 0.0 copy-done.6
  75.3 1.2 %finish.1 = bf16[128,512]{1,0:T(8,128)(2,1)S(1)} custom-call(s32[1]{0:T(128)} %bitcast.me_ref, f32[4]{0:T(128)S(1)} %copy-done.6, bf16[16,144,128]{2,1,0:T(8,128)(2,1)S(1)} %all-to-all-done.got_ref, bf16[128,512]{1,0:T(8,128)(2,1)S(1)} %constant_dynamic-slice_fusion.1.x_ref, s32[1,128]{1,0:T(1,128)S(1)} %constant_dynamic-slice_fusion.kinds_ref, ...), custom_call_target="tpu_custom_call" | custom-call | tf_op jit(solution)/shard_map/finish/pallas_call | solution.py:418
  76.6 16.5 %all_gather.3 = bf16[512,512]{1,0:T(8,128)(2,1)S(1)} all-gather(bf16[128,512]{1,0:T(8,128)(2,1)S(1)} %finish.1), channel_id=1, replica_groups=mesh['rel'=4,'node'=2,'head'=4] {'rel'}, dimensions={0}, use_global_device_ids=true | all-gather | bytes 655360 | tf_op jit(solution)/shard_map/all_gather | solution.py:426
  93.1 0.8 copy.24
  (6 shorter events, 0.0 us)
Async XLA Ops:
  0.0 8.1 %copy-start.7 = (s32[16,1]{0,1:T(1,128)S(1)}, s32[16,1]{0,1:T(1,128)}, u32[]{:S(2)}) copy-start(s32[16,1]{0,1:T(1,128)} %param.29) | copy-start | bytes 196
  0.0 8.2 %copy-start.4 = (s32[16]{0:T(128)S(1)}, s32[16]{0:T(128)}, u32[]{:S(2)}) copy-start(s32[16]{0:T(128)} %perm_ref.5) | copy-start | bytes 196
  5.0 20.5 %collective-permute-start = (bf16[16,128,128]{2,1,0:T(8,128)(2,1)S(1)}, bf16[16,128,128]{2,1,0:T(8,128)(2,1)S(1)}, u32[]{:S(2)}, u32[]{:S(2)}) collective-permute-start(bf16[16,128,128]{2,1,0:T(8,128)(2,1)S(1)} %get-tuple-element.17.k_ref), channel_id=1, source_target_pairs={{0,4},{4,0},{1,5},{5,1},{2,6},{6,2},{3,7},{7,3},{8,12},{12,8},{9,1... | collective-permute-start | bytes 1572872 | tf_op jit(solution)/shard_map/ppermute | solution.py:342
  8.1 23.2 %collective-permute-start.1 = (bf16[16,128,128]{2,1,0:T(8,128)(2,1)S(1)}, bf16[16,128,128]{2,1,0:T(8,128)(2,1)S(1)}, u32[]{:S(2)}, u32[]{:S(2)}) collective-permute-start(bf16[16,128,128]{2,1,0:T(8,128)(2,1)S(1)} %get-tuple-element.18.vt_ref), channel_id=1, source_target_pairs={{0,4},{4,0},{1,5},{5,1},{2,6},{6,2},{3,7},{7,3},{8,12},{12,8},{9,1... | collective-permute-start | bytes 1572872 | tf_op jit(solution)/shard_map/ppermute | solution.py:343
  8.2 6.0 %copy-start = (s32[16,16,128,4]{2,3,1,0:T(4,128)S(1)}, s32[16,16,128,4]{2,3,1,0:T(4,128)}, u32[]{:S(2)}) copy-start(s32[16,16,128,4]{2,3,1,0:T(4,128)} %param.28) | copy-start | bytes 1572868
  8.2 6.0 %copy-start.2 = (s32[16,16]{1,0:T(8,128)S(1)}, s32[16,16]{1,0:T(8,128)}, u32[]{:S(2)}) copy-start(s32[16,16]{1,0:T(8,128)} %src_ref.1) | copy-start | bytes 3076
  8.2 6.1 %copy-start.3 = (s32[16,16]{1,0:T(8,128)S(1)}, s32[16,16]{1,0:T(8,128)}, u32[]{:S(2)}) copy-start(s32[16,16]{1,0:T(8,128)} %dst_ref.1) | copy-start | bytes 3076
  8.2 6.1 %copy-start.5 = (f32[64,2]{0,1:T(2,128)S(1)}, f32[64,2]{0,1:T(2,128)}, u32[]{:S(2)}) copy-start(f32[64,2]{0,1:T(2,128)} %param.22) | copy-start | bytes 1540
  31.2 14.3 %copy-start.1 = (bf16[4,128,512]{2,1,0:T(8,128)(2,1)S(1)}, bf16[4,128,512]{2,1,0:T(8,128)(2,1)}, u32[]{:S(2)}) copy-start(bf16[4,128,512]{2,1,0:T(8,128)(2,1)} %refs_0_.1) | copy-start | bytes 1572868
  31.2 44.1 %copy-start.6 = (f32[4]{0:T(128)S(1)}, f32[4]{0:T(128)}, u32[]{:S(2)}) copy-start(f32[4]{0:T(128)} %skip_ref.1) | copy-start | bytes 52
  40.5 34.8 %all-to-all-start = ((bf16[16,144,128]{2,1,0:T(8,128)(2,1)}), bf16[16,144,128]{2,1,0:T(8,128)(2,1)S(1)}, u32[]{:S(2)}, u32[]{:S(2)}) async-start(bf16[16,144,128]{2,1,0:T(8,128)(2,1)} %get-tuple-element.26), calls=%async_computation | async-start | bytes 1179648 | tf_op jit(solution)/shard_map/all_to_all | solution.py:413
  45.6 20.1 %collective-permute-start.2 = (bf16[4,128,512]{2,1,0:T(8,128)(2,1)S(1)}, bf16[4,128,512]{2,1,0:T(8,128)(2,1)S(1)}, u32[]{:S(2)}, u32[]{:S(2)}) collective-permute-start(bf16[4,128,512]{2,1,0:T(8,128)(2,1)S(1)} %copy-done.1), channel_id=1, source_target_pairs={{0,1},{1,2},{2,3},{3,0},{4,5},{5,6},{6,7},{7,4},{8,9},{9,10},{10,1... | collective-permute-start | bytes 1572872 | tf_op jit(solution)/shard_map/ppermute | solution.py:320
  46.0 20.8 %collective-permute-start.3 = (bf16[4,128,512]{2,1,0:T(8,128)(2,1)S(1)}, bf16[4,128,512]{2,1,0:T(8,128)(2,1)S(1)}, u32[]{:S(2)}, u32[]{:S(2)}) collective-permute-start(bf16[4,128,512]{2,1,0:T(8,128)(2,1)S(1)} %copy-done.1), channel_id=1, source_target_pairs={{0,2},{1,3},{2,0},{3,1},{4,6},{5,7},{6,4},{7,5},{8,10},{9,11},{10,... | collective-permute-start | bytes 1572872 | tf_op jit(solution)/shard_map/ppermute | solution.py:320
  47.6 27.7 %collective-permute-start.4 = (bf16[4,128,512]{2,1,0:T(8,128)(2,1)S(1)}, bf16[4,128,512]{2,1,0:T(8,128)(2,1)S(1)}, u32[]{:S(2)}, u32[]{:S(2)}) collective-permute-start(bf16[4,128,512]{2,1,0:T(8,128)(2,1)S(1)} %copy-done.1), channel_id=1, source_target_pairs={{0,3},{1,0},{2,1},{3,2},{4,7},{5,4},{6,5},{7,6},{8,11},{9,8},{10,9... | collective-permute-start | bytes 1572872 | tf_op jit(solution)/shard_map/ppermute | solution.py:320
